TPU v7x, 32 devices: a 4x4x1 block of a 4x4x8 slice. The times are simulated.
32 devices in a mesh: replica: 1 (over z), model2: 4 (over y), model: 8 (over x, core).
Axes of the slice: x: 4, y: 4, z: 1, core: 2. Of those that a mesh axis runs over, the one named last changes fastest.
The devices are a block of a 4x4x8 slice.
Arguments:
- x_prompt: bfloat16 [6, 1, 128, 2048], P('replica')
- lengths: int32 [6, 1], P('replica')
- x_new: bfloat16 [6, 2048], P('replica')
- st_qkv: bfloat16 [8, 2048, 2560], P('model')
- st_out: bfloat16 [8, 2048, 2048], P('model')
- st_gateup: bfloat16 [8, 2048, 11264], P('model')
- st_down_t: bfloat16 [8, 2048, 5632], P('model')
- gain_attn: float32 [8, 2048], replicated
- gain_mlp: float32 [8, 2048], replicated
- tp_query: bfloat16 [8, 2048, 32, 64], P(None, None, ('model', 'model2'))
- tp_key: bfloat16 [8, 2048, 32, 64], P(None, None, ('model', 'model2'))
- tp_value: bfloat16 [8, 2048, 32, 64], P(None, None, ('model', 'model2'))
- tp_out: bfloat16 [8, 32, 64, 2048], P(None, ('model', 'model2'))
- tp_gate: bfloat16 [8, 2048, 5632], P(None, None, ('model', 'model2'))
- tp_up: bfloat16 [8, 2048, 5632], P(None, None, ('model', 'model2'))
- tp_down: bfloat16 [8, 5632, 2048], P(None, ('model', 'model2'))
Outputs:
- output 1: bfloat16 [6, 2048], P('replica')
- output 2: bfloat16 [6, 2048], P('replica')
- output 3: bfloat16 [8, 6, 129, 32, 64], P(None, 'replica', None, ('model', 'model2'))
- output 4: bfloat16 [8, 6, 129, 32, 64], P(None, 'replica', None, ('model', 'model2'))
All inputs are finite; a program needn't handle non-finite values.
Results may differ from a plain program's by a relative error of at most 0.02.
Values are sent between devices in bfloat16 or wider.
A program may use at most 768 MiB of HBM per device.

v0:
```python
import jax
import jax.numpy as jnp
from jax import lax
from jax.sharding import PartitionSpec as P

EPS = 1e-5
THETA = 10000.0
TP_AXES = ('model', 'model2')


def rms_norm(values_in, gain_vec):
    x_f32 = values_in.astype(jnp.float32)
    inv_rms = lax.rsqrt(jnp.mean(x_f32 * x_f32, axis=-1, keepdims=True) + EPS)
    return (x_f32 * inv_rms * gain_vec).astype(jnp.bfloat16)


def rope_angles(positions, head_dim):
    half_dim = head_dim // 2
    inv_freq = jnp.power(THETA, jnp.arange(half_dim, dtype=jnp.float32) * (-2.0 / head_dim))
    angles = positions.astype(jnp.float32)[..., None] * inv_freq
    return jnp.cos(angles), jnp.sin(angles)


def apply_rope(values_in, cos_t, sin_t):
    half_dim = values_in.shape[-1] // 2
    first_half = values_in[..., :half_dim]
    second = values_in[..., half_dim:]
    return jnp.concatenate([first_half * cos_t - second * sin_t, second * cos_t + first_half * sin_t], axis=-1)


def stage_layer(hidden_x, key_mask, cos_t, sin_t, g_attn, g_mlp, w_qkv, w_out, w_gateup, w_down_t, head_dim):
    row_count, seq_len, model_dim = hidden_x.shape
    q_cols = w_out.shape[0]
    num_heads = q_cols // head_dim
    k_cols = (w_qkv.shape[1] - q_cols) // 2
    kv_heads = k_cols // head_dim
    group_size = num_heads // kv_heads
    ff_width = w_down_t.shape[1]
    normed = rms_norm(hidden_x, g_attn)
    proj_all = jnp.einsum('bsd,df->bsf', normed, w_qkv, preferred_element_type=jnp.float32)
    queries = apply_rope(proj_all[..., :q_cols].reshape(row_count, seq_len, kv_heads, group_size, head_dim), cos_t[None, :, None, None, :], sin_t[None, :, None, None, :]).astype(jnp.bfloat16)
    key_rot = apply_rope(proj_all[..., q_cols:q_cols + k_cols].reshape(row_count, seq_len, kv_heads, head_dim), cos_t[None, :, None, :], sin_t[None, :, None, :]).astype(jnp.bfloat16)
    val_proj = proj_all[..., q_cols + k_cols:].reshape(row_count, seq_len, kv_heads, head_dim).astype(jnp.bfloat16)
    scores = jnp.einsum('bqcge,bkce->bcgqk', queries, key_rot, preferred_element_type=jnp.float32) * head_dim ** -0.5
    scores = jnp.where(key_mask[:, None, None], scores, -1e30)
    probs_bf = jax.nn.softmax(scores, axis=-1).astype(jnp.bfloat16)
    attn_out = jnp.einsum('bcgqk,bkce->bqcge', probs_bf, val_proj, preferred_element_type=jnp.float32).astype(jnp.bfloat16).reshape(row_count, seq_len, q_cols)
    resid_mid = (hidden_x.astype(jnp.float32) + jnp.einsum('bsf,fd->bsd', attn_out, w_out, preferred_element_type=jnp.float32)).astype(jnp.bfloat16)
    normed_mlp = rms_norm(resid_mid, g_mlp)
    gate_up = jnp.einsum('bsd,df->bsf', normed_mlp, w_gateup, preferred_element_type=jnp.float32)
    act_out = (jax.nn.silu(gate_up[..., :ff_width]) * gate_up[..., ff_width:]).astype(jnp.bfloat16)
    layer_out = (resid_mid.astype(jnp.float32) + jnp.einsum('bsf,df->bsd', act_out, w_down_t, preferred_element_type=jnp.float32)).astype(jnp.bfloat16)
    return layer_out, key_rot, val_proj


def decode_stack(x_new, len_flat, gain_attn, gain_mlp, tp_query, tp_key, tp_value, tp_out, tp_gate, tp_up, tp_down, k_prompt, v_prompt):
    n_rows = x_new.shape[0]
    head_dim = tp_query.shape[-1]
    per_dev = tp_key.shape[2]
    group_size = tp_query.shape[2] // per_dev
    seq_len = k_prompt.shape[2]
    cos_n, sin_n = rope_angles(len_flat, head_dim)
    cached = jnp.arange(seq_len)[None, :] < len_flat[:, None]
    score_scale = head_dim ** -0.5

    def layer_fn(carry_x, params):
        g_attn, g_mlp, w_query, w_key, w_value, w_outp, w_gate, w_upp, w_down, k_cached, v_cached = params
        normed = rms_norm(carry_x, g_attn)
        queries = apply_rope(jnp.einsum('bd,dhe->bhe', normed, w_query, preferred_element_type=jnp.float32), cos_n[:, None, :], sin_n[:, None, :])
        queries = queries.astype(jnp.bfloat16).reshape(n_rows, per_dev, group_size, head_dim)
        key_new = apply_rope(jnp.einsum('bd,dce->bce', normed, w_key, preferred_element_type=jnp.float32), cos_n[:, None, :], sin_n[:, None, :]).astype(jnp.bfloat16)
        val_new = jnp.einsum('bd,dce->bce', normed, w_value, preferred_element_type=jnp.float32).astype(jnp.bfloat16)
        s_old = jnp.einsum('bcge,bsce->bcgs', queries, k_cached, preferred_element_type=jnp.float32) * score_scale
        s_old = jnp.where(cached[:, None, None, :], s_old, -1e30)
        s_new = jnp.einsum('bcge,bce->bcg', queries, key_new, preferred_element_type=jnp.float32) * score_scale
        row_max = jnp.maximum(jnp.max(s_old, axis=-1), s_new)
        e_old = jnp.exp(s_old - row_max[..., None])
        e_new = jnp.exp(s_new - row_max)
        denom_sum = jnp.sum(e_old, axis=-1) + e_new
        p_old = (e_old / denom_sum[..., None]).astype(jnp.bfloat16)
        p_new = (e_new / denom_sum).astype(jnp.bfloat16)
        attn_out = jnp.einsum('bcgs,bsce->bcge', p_old, v_cached, preferred_element_type=jnp.float32) + p_new.astype(jnp.float32)[..., None] * val_new.astype(jnp.float32)[:, :, None, :]
        attn_out = attn_out.astype(jnp.bfloat16).reshape(n_rows, per_dev * group_size, head_dim)
        part_sum = lax.psum(jnp.einsum('bhe,hed->bd', attn_out, w_outp, preferred_element_type=jnp.float32), TP_AXES)
        resid_mid = (carry_x.astype(jnp.float32) + part_sum).astype(jnp.bfloat16)
        normed_mlp = rms_norm(resid_mid, g_mlp)
        act_out = (jax.nn.silu(jnp.dot(normed_mlp, w_gate, preferred_element_type=jnp.float32)) * jnp.dot(normed_mlp, w_upp, preferred_element_type=jnp.float32)).astype(jnp.bfloat16)
        down_sum = lax.psum(jnp.dot(act_out, w_down, preferred_element_type=jnp.float32), TP_AXES)
        layer_out = (resid_mid.astype(jnp.float32) + down_sum).astype(jnp.bfloat16)
        return layer_out, (key_new, val_new)

    dec_out, new_kv = lax.scan(layer_fn, x_new, (gain_attn, gain_mlp, tp_query, tp_key, tp_value, tp_out, tp_gate, tp_up, tp_down, k_prompt, v_prompt))
    k_full = jnp.concatenate([k_prompt, new_kv[0][:, :, None]], axis=2)
    v_full = jnp.concatenate([v_prompt, new_kv[1][:, :, None]], axis=2)
    return dec_out, k_full, v_full


def solution(mesh):
    stages = mesh.shape['model']
    width = mesh.shape['model2']
    stage_spec = P('model', None, None)
    in_specs = (P('replica', None, None, None), P('replica', None), P('replica', None),
                stage_spec, stage_spec, stage_spec, stage_spec, P(None, None), P(None, None),
                P(None, None, TP_AXES, None), P(None, None, TP_AXES, None), P(None, None, TP_AXES, None),
                P(None, TP_AXES, None, None), P(None, None, TP_AXES), P(None, None, TP_AXES), P(None, TP_AXES, None))
    cache_spec = P(None, 'replica', None, TP_AXES, None)
    out_specs = (P('replica', None), P('replica', None), cache_spec, cache_spec)

    def shard_body(x_prompt, lengths, x_new, st_qkv, st_out, st_gateup, st_down_t, gain_attn, gain_mlp, tp_query, tp_key, tp_value, tp_out, tp_gate, tp_up, tp_down):
        num_micro, row_count, seq_len, model_dim = x_prompt.shape
        batch_rows = num_micro * row_count
        stage_layers = st_qkv.shape[0]
        head_dim = tp_query.shape[-1]
        q_cols = st_out.shape[1]
        kv_heads = (st_qkv.shape[2] - q_cols) // (2 * head_dim)
        per_dev = tp_key.shape[2]
        num_slots = per_dev * stages * width
        stage_idx = lax.axis_index('model')
        col_idx = lax.axis_index('model2')
        stage_g_attn = lax.dynamic_slice_in_dim(gain_attn, stage_idx * stage_layers, stage_layers, 0)
        stage_g_mlp = lax.dynamic_slice_in_dim(gain_mlp, stage_idx * stage_layers, stage_layers, 0)
        positions = jnp.arange(seq_len)
        cos_t, sin_t = rope_angles(positions, head_dim)
        causal = positions[None, :] <= positions[:, None]
        send_pairs = [(i, i + 1) for i in range(stages - 1)]

        def tick_fn(carry, tick_idx):
            recv_act, k_store, v_store, last_rows = carry
            mb_raw = tick_idx - stage_idx
            is_valid = (mb_raw >= 0) & (mb_raw < num_micro)
            mb_idx = jnp.clip(mb_raw, 0, num_micro - 1)
            fresh_act = lax.dynamic_index_in_dim(x_prompt, mb_idx, 0, keepdims=False)
            hidden_x = jnp.where(stage_idx == 0, fresh_act, recv_act)
            len_mb = lax.dynamic_index_in_dim(lengths, mb_idx, 0, keepdims=False)
            key_mask = causal[None] & (positions[None, None, :] < len_mb[:, None, None])
            row_start = mb_idx * row_count
            for layer_idx in range(stage_layers):
                hidden_x, key_rot, val_proj = stage_layer(hidden_x, key_mask, cos_t, sin_t, stage_g_attn[layer_idx], stage_g_mlp[layer_idx], st_qkv[layer_idx], st_out[layer_idx], st_gateup[layer_idx], st_down_t[layer_idx], head_dim)
                corner = (layer_idx, row_start, 0, 0, 0)
                block = (1, row_count, seq_len, kv_heads, head_dim)
                k_store = lax.dynamic_update_slice(k_store, jnp.where(is_valid, key_rot[None], lax.dynamic_slice(k_store, corner, block)), corner)
                v_store = lax.dynamic_update_slice(v_store, jnp.where(is_valid, val_proj[None], lax.dynamic_slice(v_store, corner, block)), corner)
            picked = jnp.take_along_axis(hidden_x, (len_mb - 1)[:, None, None], axis=1)[:, 0]
            old_rows = lax.dynamic_slice_in_dim(last_rows, row_start, row_count, 0)
            keep_last = is_valid & (stage_idx == stages - 1)
            last_rows = lax.dynamic_update_slice_in_dim(last_rows, jnp.where(keep_last, picked, old_rows), row_start, 0)
            recv_act = lax.ppermute(hidden_x, 'model', send_pairs)
            return (recv_act, k_store, v_store, last_rows), None

        kv_shape = (stage_layers, batch_rows, seq_len, kv_heads, head_dim)
        init_carry = (jnp.zeros((row_count, seq_len, model_dim), jnp.bfloat16), jnp.zeros(kv_shape, jnp.bfloat16), jnp.zeros(kv_shape, jnp.bfloat16), jnp.zeros((batch_rows, model_dim), jnp.bfloat16))
        final_carry = lax.scan(tick_fn, init_carry, jnp.arange(num_micro + stages - 1))[0]
        last_hidden = lax.psum(final_carry[3], 'model')

        def regroup(store):
            wide_view = jnp.broadcast_to(store[:, :, :, :, None, :], (stage_layers, batch_rows, seq_len, kv_heads, num_slots // kv_heads, head_dim))
            wide_view = wide_view.reshape(stage_layers, batch_rows, seq_len, stages, width, per_dev, head_dim)
            mine_sel = lax.dynamic_index_in_dim(wide_view, col_idx, axis=4, keepdims=False)
            moved_kv = lax.all_to_all(mine_sel, 'model', 3, 0, tiled=True)
            return moved_kv.reshape(stages * stage_layers, batch_rows, seq_len, per_dev, head_dim)

        k_mine = regroup(final_carry[1])
        v_mine = regroup(final_carry[2])
        dec_out, k_full, v_full = decode_stack(x_new, lengths.reshape(batch_rows), gain_attn, gain_mlp, tp_query, tp_key, tp_value, tp_out, tp_gate, tp_up, tp_down, k_mine, v_mine)
        return dec_out, last_hidden, k_full, v_full

    return jax.shard_map(shard_body, mesh=mesh, in_specs=in_specs, out_specs=out_specs, check_vma=False)
```

profile of v0, /device:TPU:97, one launch (start us, length us, event | category | flops | bytes accessed | tf_op | source)
XLA Modules:
  0.0 1663.7 jit_solution(14606066735915274563)
XLA Ops:
  3.3 794.2 %while.39 = (s32[]{:T(128)}, bf16[1,128,2048]{2,1,0:T(8,128)(2,1)S(1)}, bf16[1,6,128,4,64]{2,4,3,1,0:T(8,128)(2,1)}, bf16[1,6,128,4,64]{2,4,3,1,0:T(8,128)(2,1)}...) while((s32[]{:T(128)}, ...), condition=%wide.region_5.6_spmd.clone.clone.clone, body=%wide.region_0.5_spmd.clone.clone.clone.sunk | while | flops 11424858112 | bytes 124708264 | solution.py:152
  6.0 5.6 fusion.257
  20.3 20.0 %fusion.263 = f32[1,128,11264]{2,1,0:T(8,128)} fusion(bf16[1,2048,11264]{2,1,0:T(8,128)(2,1)} %get-tuple-element.1137, f32[1,128,2048]{2,1,0:T(8,128)S(1)} %get-tuple-element.1066, f32[2048]{0:T(1024)S(1)} %bitcast.392, f32[128]{0:T(128)S(1)} %add_rsqrt_fusion.11), kind=kOutput, calls=%fused_computation.11.clone.1 | convolution fusion | flops 5906366464 | bytes 52961792 | tf_op jit(solution)/shard_map/while/body/eval_jaxpr/bsd,df->bsf/dot_general | solution.py:50
  40.3 13.6 fusion.264
  81.5 20.0 %fusion.263 = f32[1,128,11264]{2,1,0:T(8,128)} fusion(bf16[1,2048,11264]{2,1,0:T(8,128)(2,1)} %get-tuple-element.1137, f32[1,128,2048]{2,1,0:T(8,128)S(1)} %get-tuple-element.1066, f32[2048]{0:T(1024)S(1)} %bitcast.392, f32[128]{0:T(128)S(1)} %add_rsqrt_fusion.11), kind=kOutput, calls=%fused_computation.11.clone.1 | convolution fusion | flops 5906366464 | bytes 52961792 | tf_op jit(solution)/shard_map/while/body/eval_jaxpr/bsd,df->bsf/dot_general | solution.py:50
  101.5 13.6 fusion.264
  142.6 20.0 %fusion.263 = f32[1,128,11264]{2,1,0:T(8,128)} fusion(bf16[1,2048,11264]{2,1,0:T(8,128)(2,1)} %get-tuple-element.1137, f32[1,128,2048]{2,1,0:T(8,128)S(1)} %get-tuple-element.1066, f32[2048]{0:T(1024)S(1)} %bitcast.392, f32[128]{0:T(128)S(1)} %add_rsqrt_fusion.11), kind=kOutput, calls=%fused_computation.11.clone.1 | convolution fusion | flops 5906366464 | bytes 52961792 | tf_op jit(solution)/shard_map/while/body/eval_jaxpr/bsd,df->bsf/dot_general | solution.py:50
  162.6 13.6 fusion.264
  203.7 20.0 %fusion.263 = f32[1,128,11264]{2,1,0:T(8,128)} fusion(bf16[1,2048,11264]{2,1,0:T(8,128)(2,1)} %get-tuple-element.1137, f32[1,128,2048]{2,1,0:T(8,128)S(1)} %get-tuple-element.1066, f32[2048]{0:T(1024)S(1)} %bitcast.392, f32[128]{0:T(128)S(1)} %add_rsqrt_fusion.11), kind=kOutput, calls=%fused_computation.11.clone.1 | convolution fusion | flops 5906366464 | bytes 52961792 | tf_op jit(solution)/shard_map/while/body/eval_jaxpr/bsd,df->bsf/dot_general | solution.py:50
  223.6 13.6 fusion.264
  264.8 20.0 %fusion.263 = f32[1,128,11264]{2,1,0:T(8,128)} fusion(bf16[1,2048,11264]{2,1,0:T(8,128)(2,1)} %get-tuple-element.1137, f32[1,128,2048]{2,1,0:T(8,128)S(1)} %get-tuple-element.1066, f32[2048]{0:T(1024)S(1)} %bitcast.392, f32[128]{0:T(128)S(1)} %add_rsqrt_fusion.11), kind=kOutput, calls=%fused_computation.11.clone.1 | convolution fusion | flops 5906366464 | bytes 52961792 | tf_op jit(solution)/shard_map/while/body/eval_jaxpr/bsd,df->bsf/dot_general | solution.py:50
  284.7 13.6 fusion.264
  325.8 20.0 %fusion.263 = f32[1,128,11264]{2,1,0:T(8,128)} fusion(bf16[1,2048,11264]{2,1,0:T(8,128)(2,1)} %get-tuple-element.1137, f32[1,128,2048]{2,1,0:T(8,128)S(1)} %get-tuple-element.1066, f32[2048]{0:T(1024)S(1)} %bitcast.392, f32[128]{0:T(128)S(1)} %add_rsqrt_fusion.11), kind=kOutput, calls=%fused_computation.11.clone.1 | convolution fusion | flops 5906366464 | bytes 52961792 | tf_op jit(solution)/shard_map/while/body/eval_jaxpr/bsd,df->bsf/dot_general | solution.py:50
  345.8 13.6 fusion.264
  386.9 20.0 %fusion.263 = f32[1,128,11264]{2,1,0:T(8,128)} fusion(bf16[1,2048,11264]{2,1,0:T(8,128)(2,1)} %get-tuple-element.1137, f32[1,128,2048]{2,1,0:T(8,128)S(1)} %get-tuple-element.1066, f32[2048]{0:T(1024)S(1)} %bitcast.392, f32[128]{0:T(128)S(1)} %add_rsqrt_fusion.11), kind=kOutput, calls=%fused_computation.11.clone.1 | convolution fusion | flops 5906366464 | bytes 52961792 | tf_op jit(solution)/shard_map/while/body/eval_jaxpr/bsd,df->bsf/dot_general | solution.py:50
  406.9 13.6 fusion.264
  448.0 20.0 %fusion.263 = f32[1,128,11264]{2,1,0:T(8,128)} fusion(bf16[1,2048,11264]{2,1,0:T(8,128)(2,1)} %get-tuple-element.1137, f32[1,128,2048]{2,1,0:T(8,128)S(1)} %get-tuple-element.1066, f32[2048]{0:T(1024)S(1)} %bitcast.392, f32[128]{0:T(128)S(1)} %add_rsqrt_fusion.11), kind=kOutput, calls=%fused_computation.11.clone.1 | convolution fusion | flops 5906366464 | bytes 52961792 | tf_op jit(solution)/shard_map/while/body/eval_jaxpr/bsd,df->bsf/dot_general | solution.py:50
  468.0 13.6 fusion.264
  509.1 20.0 %fusion.263 = f32[1,128,11264]{2,1,0:T(8,128)} fusion(bf16[1,2048,11264]{2,1,0:T(8,128)(2,1)} %get-tuple-element.1137, f32[1,128,2048]{2,1,0:T(8,128)S(1)} %get-tuple-element.1066, f32[2048]{0:T(1024)S(1)} %bitcast.392, f32[128]{0:T(128)S(1)} %add_rsqrt_fusion.11), kind=kOutput, calls=%fused_computation.11.clone.1 | convolution fusion | flops 5906366464 | bytes 52961792 | tf_op jit(solution)/shard_map/while/body/eval_jaxpr/bsd,df->bsf/dot_general | solution.py:50
  529.0 13.6 fusion.264
  570.1 20.0 %fusion.263 = f32[1,128,11264]{2,1,0:T(8,128)} fusion(bf16[1,2048,11264]{2,1,0:T(8,128)(2,1)} %get-tuple-element.1137, f32[1,128,2048]{2,1,0:T(8,128)S(1)} %get-tuple-element.1066, f32[2048]{0:T(1024)S(1)} %bitcast.392, f32[128]{0:T(128)S(1)} %add_rsqrt_fusion.11), kind=kOutput, calls=%fused_computation.11.clone.1 | convolution fusion | flops 5906366464 | bytes 52961792 | tf_op jit(solution)/shard_map/while/body/eval_jaxpr/bsd,df->bsf/dot_general | solution.py:50
  590.1 13.6 fusion.264
  631.2 20.0 %fusion.263 = f32[1,128,11264]{2,1,0:T(8,128)} fusion(bf16[1,2048,11264]{2,1,0:T(8,128)(2,1)} %get-tuple-element.1137, f32[1,128,2048]{2,1,0:T(8,128)S(1)} %get-tuple-element.1066, f32[2048]{0:T(1024)S(1)} %bitcast.392, f32[128]{0:T(128)S(1)} %add_rsqrt_fusion.11), kind=kOutput, calls=%fused_computation.11.clone.1 | convolution fusion | flops 5906366464 | bytes 52961792 | tf_op jit(solution)/shard_map/while/body/eval_jaxpr/bsd,df->bsf/dot_general | solution.py:50
  651.2 13.6 fusion.264
  692.3 20.0 %fusion.263 = f32[1,128,11264]{2,1,0:T(8,128)} fusion(bf16[1,2048,11264]{2,1,0:T(8,128)(2,1)} %get-tuple-element.1137, f32[1,128,2048]{2,1,0:T(8,128)S(1)} %get-tuple-element.1066, f32[2048]{0:T(1024)S(1)} %bitcast.392, f32[128]{0:T(128)S(1)} %add_rsqrt_fusion.11), kind=kOutput, calls=%fused_computation.11.clone.1 | convolution fusion | flops 5906366464 | bytes 52961792 | tf_op jit(solution)/shard_map/while/body/eval_jaxpr/bsd,df->bsf/dot_general | solution.py:50
  712.3 13.6 fusion.264
  753.4 20.0 %fusion.263 = f32[1,128,11264]{2,1,0:T(8,128)} fusion(bf16[1,2048,11264]{2,1,0:T(8,128)(2,1)} %get-tuple-element.1137, f32[1,128,2048]{2,1,0:T(8,128)S(1)} %get-tuple-element.1066, f32[2048]{0:T(1024)S(1)} %bitcast.392, f32[128]{0:T(128)S(1)} %add_rsqrt_fusion.11), kind=kOutput, calls=%fused_computation.11.clone.1 | convolution fusion | flops 5906366464 | bytes 52961792 | tf_op jit(solution)/shard_map/while/body/eval_jaxpr/bsd,df->bsf/dot_general | solution.py:50
  773.3 13.6 fusion.264
  799.7 6.0 all-to-all-start.1
  805.7 11.9 all-to-all-done.1
  823.4 26.5 %psum.21 = bf16[6,2048]{1,0:T(8,128)(2,1)} all-reduce(bf16[6,2048]{1,0:T(8,128)(2,1)S(1)} %get-tuple-element.365), channel_id=1, replica_groups=mesh['replica'=1,'model2'=4,'model'=8] {'model'}, use_global_device_ids=true, to_apply=%region_14.15 | all-reduce | flops 12288 | bytes 49152 | tf_op jit(solution)/shard_map/psum | solution.py:153
  849.9 809.6 %while.38 = (s32[]{:T(128)}, bf16[6,2048]{1,0:T(8,128)(2,1)S(1)}, bf16[8,6,1,64]{3,1,2,0:T(8,128)(2,1)S(1)}, bf16[8,6,1,64]{3,1,2,0:T(8,128)(2,1)S(1)}, f32[8,20...) while((s32[]{:T(128)}, bf16[6,2048]{1,0:T(8,128)(2,1)S(1)}, ...), condition=%wide.region_13.14_spmd.clone.clone, body=%wide.region_6.13_spmd.clone.clone.sunk | while | flops 19911984 | bytes 4183569 | solution.py:92
  857.8 49.9 %psum.28 = f32[6,2048]{1,0:T(8,128)S(1)} all-reduce(f32[6,2048]{1,0:T(8,128)S(1)} %fusion.242), channel_id=1, replica_groups=mesh['replica'=1,'model2'=4,'model'=8] {'model','model2'}, use_global_device_ids=true, to_apply=%region_10.10 | all-reduce | flops 12288 | bytes 98304 | tf_op jit(solution)/shard_map/while/body/eval_jaxpr/psum | solution.py:84
  911.3 43.9 %psum.29 = f32[6,2048]{1,0:T(8,128)S(1)} all-reduce(f32[6,2048]{1,0:T(8,128)S(1)} %fusion.245), channel_id=1, replica_groups=mesh['replica'=1,'model2'=4,'model'=8] {'model','model2'}, use_global_device_ids=true, to_apply=%region_12.12 | all-reduce | flops 12288 | bytes 98304 | tf_op jit(solution)/shard_map/while/body/eval_jaxpr/psum | solution.py:88
  963.0 44.0 %psum.28 = f32[6,2048]{1,0:T(8,128)S(1)} all-reduce(f32[6,2048]{1,0:T(8,128)S(1)} %fusion.242), channel_id=1, replica_groups=mesh['replica'=1,'model2'=4,'model'=8] {'model','model2'}, use_global_device_ids=true, to_apply=%region_10.10 | all-reduce | flops 12288 | bytes 98304 | tf_op jit(solution)/shard_map/while/body/eval_jaxpr/psum | solution.py:84
  1010.6 44.5 %psum.29 = f32[6,2048]{1,0:T(8,128)S(1)} all-reduce(f32[6,2048]{1,0:T(8,128)S(1)} %fusion.245), channel_id=1, replica_groups=mesh['replica'=1,'model2'=4,'model'=8] {'model','model2'}, use_global_device_ids=true, to_apply=%region_12.12 | all-reduce | flops 12288 | bytes 98304 | tf_op jit(solution)/shard_map/while/body/eval_jaxpr/psum | solution.py:88
  1063.0 44.6 %psum.28 = f32[6,2048]{1,0:T(8,128)S(1)} all-reduce(f32[6,2048]{1,0:T(8,128)S(1)} %fusion.242), channel_id=1, replica_groups=mesh['replica'=1,'model2'=4,'model'=8] {'model','model2'}, use_global_device_ids=true, to_apply=%region_10.10 | all-reduce | flops 12288 | bytes 98304 | tf_op jit(solution)/shard_map/while/body/eval_jaxpr/psum | solution.py:84
  1111.1 44.7 %psum.29 = f32[6,2048]{1,0:T(8,128)S(1)} all-reduce(f32[6,2048]{1,0:T(8,128)S(1)} %fusion.245), channel_id=1, replica_groups=mesh['replica'=1,'model2'=4,'model'=8] {'model','model2'}, use_global_device_ids=true, to_apply=%region_12.12 | all-reduce | flops 12288 | bytes 98304 | tf_op jit(solution)/shard_map/while/body/eval_jaxpr/psum | solution.py:88
  1163.7 44.6 %psum.28 = f32[6,2048]{1,0:T(8,128)S(1)} all-reduce(f32[6,2048]{1,0:T(8,128)S(1)} %fusion.242), channel_id=1, replica_groups=mesh['replica'=1,'model2'=4,'model'=8] {'model','model2'}, use_global_device_ids=true, to_apply=%region_10.10 | all-reduce | flops 12288 | bytes 98304 | tf_op jit(solution)/shard_map/while/body/eval_jaxpr/psum | solution.py:84
  1211.9 44.7 %psum.29 = f32[6,2048]{1,0:T(8,128)S(1)} all-reduce(f32[6,2048]{1,0:T(8,128)S(1)} %fusion.245), channel_id=1, replica_groups=mesh['replica'=1,'model2'=4,'model'=8] {'model','model2'}, use_global_device_ids=true, to_apply=%region_12.12 | all-reduce | flops 12288 | bytes 98304 | tf_op jit(solution)/shard_map/while/body/eval_jaxpr/psum | solution.py:88
  1264.5 44.6 %psum.28 = f32[6,2048]{1,0:T(8,128)S(1)} all-reduce(f32[6,2048]{1,0:T(8,128)S(1)} %fusion.242), channel_id=1, replica_groups=mesh['replica'=1,'model2'=4,'model'=8] {'model','model2'}, use_global_device_ids=true, to_apply=%region_10.10 | all-reduce | flops 12288 | bytes 98304 | tf_op jit(solution)/shard_map/while/body/eval_jaxpr/psum | solution.py:84
  1312.6 44.7 %psum.29 = f32[6,2048]{1,0:T(8,128)S(1)} all-reduce(f32[6,2048]{1,0:T(8,128)S(1)} %fusion.245), channel_id=1, replica_groups=mesh['replica'=1,'model2'=4,'model'=8] {'model','model2'}, use_global_device_ids=true, to_apply=%region_12.12 | all-reduce | flops 12288 | bytes 98304 | tf_op jit(solution)/shard_map/while/body/eval_jaxpr/psum | solution.py:88
  1365.2 44.6 %psum.28 = f32[6,2048]{1,0:T(8,128)S(1)} all-reduce(f32[6,2048]{1,0:T(8,128)S(1)} %fusion.242), channel_id=1, replica_groups=mesh['replica'=1,'model2'=4,'model'=8] {'model','model2'}, use_global_device_ids=true, to_apply=%region_10.10 | all-reduce | flops 12288 | bytes 98304 | tf_op jit(solution)/shard_map/while/body/eval_jaxpr/psum | solution.py:84
  1413.4 44.7 %psum.29 = f32[6,2048]{1,0:T(8,128)S(1)} all-reduce(f32[6,2048]{1,0:T(8,128)S(1)} %fusion.245), channel_id=1, replica_groups=mesh['replica'=1,'model2'=4,'model'=8] {'model','model2'}, use_global_device_ids=true, to_apply=%region_12.12 | all-reduce | flops 12288 | bytes 98304 | tf_op jit(solution)/shard_map/while/body/eval_jaxpr/psum | solution.py:88
  1465.9 44.6 %psum.28 = f32[6,2048]{1,0:T(8,128)S(1)} all-reduce(f32[6,2048]{1,0:T(8,128)S(1)} %fusion.242), channel_id=1, replica_groups=mesh['replica'=1,'model2'=4,'model'=8] {'model','model2'}, use_global_device_ids=true, to_apply=%region_10.10 | all-reduce | flops 12288 | bytes 98304 | tf_op jit(solution)/shard_map/while/body/eval_jaxpr/psum | solution.py:84
  1514.1 44.7 %psum.29 = f32[6,2048]{1,0:T(8,128)S(1)} all-reduce(f32[6,2048]{1,0:T(8,128)S(1)} %fusion.245), channel_id=1, replica_groups=mesh['replica'=1,'model2'=4,'model'=8] {'model','model2'}, use_global_device_ids=true, to_apply=%region_12.12 | all-reduce | flops 12288 | bytes 98304 | tf_op jit(solution)/shard_map/while/body/eval_jaxpr/psum | solution.py:88
  1566.7 44.6 %psum.28 = f32[6,2048]{1,0:T(8,128)S(1)} all-reduce(f32[6,2048]{1,0:T(8,128)S(1)} %fusion.242), channel_id=1, replica_groups=mesh['replica'=1,'model2'=4,'model'=8] {'model','model2'}, use_global_device_ids=true, to_apply=%region_10.10 | all-reduce | flops 12288 | bytes 98304 | tf_op jit(solution)/shard_map/while/body/eval_jaxpr/psum | solution.py:84
  1614.8 44.7 %psum.29 = f32[6,2048]{1,0:T(8,128)S(1)} all-reduce(f32[6,2048]{1,0:T(8,128)S(1)} %fusion.245), channel_id=1, replica_groups=mesh['replica'=1,'model2'=4,'model'=8] {'model','model2'}, use_global_device_ids=true, to_apply=%region_12.12 | all-reduce | flops 12288 | bytes 98304 | tf_op jit(solution)/shard_map/while/body/eval_jaxpr/psum | solution.py:88
  (584 shorter events, 424.5 us)
Async XLA Ops:
  6.0 5.7 copy-start.3
  53.9 10.7 collective-permute-start
  67.2 5.7 copy-start.3
  115.1 10.5 collective-permute-start
  128.3 5.7 copy-start.3
  176.2 10.5 collective-permute-start
  189.4 5.7 copy-start.3
  237.3 10.5 collective-permute-start
  250.5 5.7 copy-start.3
  298.4 10.5 collective-permute-start
  311.6 5.7 copy-start.3
  359.4 10.5 collective-permute-start
  372.6 5.7 copy-start.3
  420.5 10.5 collective-permute-start
  433.7 5.7 copy-start.3
  481.6 10.5 collective-permute-start
  494.8 5.7 copy-start.3
  542.7 10.5 collective-permute-start
  555.9 5.7 copy-start.3
  603.7 10.5 collective-permute-start
  617.0 5.7 copy-start.3
  664.8 10.5 collective-permute-start
  678.0 5.7 copy-start.3
  725.9 10.5 collective-permute-start
  739.1 5.7 copy-start.3
  787.0 10.5 collective-permute-start
  797.5 8.2 copy-start.2
  799.7 50.2 %copy-start.4 = (s32[6,1]{0,1:T(1,128)S(1)}, s32[6,1]{0,1:T(1,128)}, u32[]{:S(2)}) copy-start(s32[6,1]{0,1:T(1,128)} %get-tuple-element.1211) | copy-start | bytes 76
  799.7 50.2 %copy-start.1 = (bf16[6,2048]{1,0:T(8,128)(2,1)S(1)}, bf16[6,2048]{1,0:T(8,128)(2,1)}, u32[]{:S(2)}) copy-start(bf16[6,2048]{1,0:T(8,128)(2,1)} %param.22) | copy-start | bytes 73732
  799.7 17.9 %all-to-all-start.1 = ((bf16[1,6,128,8,1,64]{2,5,1,4,0,3:T(8,128)(2,1)}), bf16[1,6,128,8,1,64]{2,5,1,4,0,3:T(8,128)(2,1)S(1)}, u32[]{:S(2)}, u32[]{:S(2)}) async-start(bf16[1,6,128,8,1,64]{2,5,1,4,0,3:T(8,128)(2,1)} %bitcast.7), calls=%async_computation.1 | async-start | bytes 1572864 | tf_op jit(solution)/shard_map/all_to_all | solution.py:159
  818.7 31.2 %all-to-all-start = ((bf16[1,6,128,8,1,64]{2,5,1,4,0,3:T(8,128)(2,1)}), bf16[1,6,128,8,1,64]{2,5,1,4,0,3:T(8,128)(2,1)S(1)}, u32[]{:S(2)}, u32[]{:S(2)}) async-start(bf16[1,6,128,8,1,64]{2,5,1,4,0,3:T(8,128)(2,1)} %bitcast.1), calls=%async_computation | async-start | bytes 1572864 | tf_op jit(solution)/shard_map/all_to_all | solution.py:159
  1659.5 4.1 copy-start
where the time goes:
time: 1670 us; the launch traced here: 1660 us
  blocking collectives  744 us (45%)
  matrix products  652 us (39%)
  other arithmetic  79.1 us (5%)
  starting transfers between devices  68.4 us (4%)
  waiting for transfers between devices  46.2 us (3%)
  local copies, waits for them, and re-layouts  38.8 us (2%)
  loops' own time  33.8 us (2%)
    psum x8, blocking collectives, layer_fn(): lax.psum(jnp.einsum('bhe,hed->bd', attn_out, w_outp, preferred_element_ty...  361 us
    psum x8, blocking collectives, layer_fn(): lax.psum(jnp.dot(act_out, w_down, preferred_element_type=jnp.float32), TP...  357 us
    dot_general x13, matrix products, stage_layer(): jnp.einsum('bsd,df->bsf', normed_mlp, w_gateup, preferred_element_type=jn...  260 us
    dot_general x13, matrix products, stage_layer(): jnp.einsum('bsf,df->bsd', act_out, w_down_t, preferred_element_type=jnp.f...  177 us
    dot_general x13, matrix products, stage_layer(): jnp.einsum('bsd,df->bsf', normed, w_qkv, preferred_element_type=jnp.float32)  72.3 us
    dot_general x13, matrix products, stage_layer(): jnp.einsum('bsf,fd->bsd', attn_out, w_out, preferred_element_type=jnp.flo...  61.9 us
    ppermute x13, starting transfers between devices, tick_fn(): recv_act = lax.ppermute(hidden_x, 'model', send_pairs)  57.7 us
    ppermute x13, waiting for transfers between devices, tick_fn(): recv_act = lax.ppermute(hidden_x, 'model', send_pairs)  34.3 us
  transfers between devices with their start and end apart: 15, of which 14 were waited for; matrix products, arithmetic and copies ran while one was open for 1% of the time, Pallas kernels for 0%

commit v1 on v0

v1 whole, which is shorter than its diff:
```python
import functools

import jax
import jax.numpy as jnp
from jax import lax
from jax.experimental import pallas as pl
from jax.experimental.pallas import tpu as pltpu
from jax.sharding import PartitionSpec as P

EPS = 1e-5
THETA = 10000.0
TP_AXES = ('model', 'model2')
MESH = pl.DeviceIdType.MESH
BLK = 256
LANES = 128
NSLOT = 50
NEG = -1e30


def rope_angles(positions, head_dim):
    half_dim = head_dim // 2
    inv_freq = jnp.power(THETA, jnp.arange(half_dim, dtype=jnp.float32) * (-2.0 / head_dim))
    angles = positions.astype(jnp.float32)[..., None] * inv_freq
    return jnp.cos(angles), jnp.sin(angles)


def dot_nn(a, b):
    return lax.dot_general(a, b, (((1,), (0,)), ((), ())), preferred_element_type=jnp.float32)


def dot_nt(a, b):
    return lax.dot_general(a, b, (((1,), (1,)), ((), ())), preferred_element_type=jnp.float32)


def stage_kernel(dims, x_hbm, dec_hbm, cos_ref, sin_ref, mask_a_ref, mask_b_ref, sel_ref, ga_ref, gm_ref,
                 w_qkv, w_out, w_gu, w_dt, kv_out, res_out,
                 ring, xin, xout, hbuf, qbuf, x1buf, abuf, kvp, kva, kvb, kv_recv, res_vm,
                 ring_sem, x0_sem, xs_sem, xr_sem, ks_sem, kr_sem, rs_sem, rr_sem, pair_sem):
    stages, width, kv_heads, head_dim, seq_a, seq_b, n_dec, q_cols, ff = dims
    n_rows = seq_a + n_dec + seq_b
    row_b = seq_a + n_dec
    d_model = w_out.shape[2]
    nx = d_model // BLK
    nq = q_cols // BLK
    nff = ff // BLK
    n_dev = stages * width
    per_head = stages // kv_heads
    stage = lax.axis_index('model')
    col = lax.axis_index('model2')
    me = stage * width + col
    half = lax.rem(col, 2)

    def ring_copy(src, slot):
        return pltpu.make_async_copy(src, ring.at[slot], ring_sem.at[slot])

    def cols(ref, c):
        return ref.at[0, :, pl.ds(pl.multiple_of(c * BLK, BLK), BLK)]

    def wait_slot(slot):
        ring_copy(cols(w_out, 0), slot).wait()

    order = [(w_qkv, nq), (w_qkv, nq + 1)] + [(w_qkv, c) for c in range(nq)] + [(w_out, c) for c in range(nx)]
    n_attn = len(order)
    for j in range(nff):
        order += [(w_gu, j), (w_gu, nff + j)]
    n_up = len(order)
    order += [(w_dt, c) for c in range(nff)]

    def issue(i):
        ref, c = order[i]
        ring_copy(cols(ref, c), i % NSLOT).start()

    for i in range(NSLOT):
        issue(i)

    barrier = pltpu.get_barrier_semaphore()

    def greet(d, carry):
        @pl.when(d != me)
        def _():
            pl.semaphore_signal(barrier, inc=1, device_id={'model': d // width, 'model2': lax.rem(d, width)}, device_id_type=MESH)
        return carry

    lax.fori_loop(0, n_dev, greet, 0)
    pl.semaphore_wait(barrier, n_dev - 1)

    @pl.when(stage == 0)
    def _():
        copies = []
        for n in range(nx):
            cs = pl.ds(n * BLK, BLK)
            copies.append(pltpu.make_async_copy(x_hbm.at[col, 0, :, cs], xin.at[n, pl.ds(0, seq_a), :], x0_sem.at[3 * n]))
            copies.append(pltpu.make_async_copy(dec_hbm.at[:, cs], xin.at[n, pl.ds(seq_a, n_dec), :], x0_sem.at[3 * n + 1]))
            copies.append(pltpu.make_async_copy(x_hbm.at[width + col // 2, 0, pl.ds(pl.multiple_of(half * seq_b, seq_b), seq_b), cs], xin.at[n, pl.ds(row_b, seq_b), :], x0_sem.at[3 * n + 2]))
        for c in copies:
            c.start()
        for c in copies:
            c.wait()

    def x_send(n):
        return pltpu.make_async_remote_copy(src_ref=xout.at[n], dst_ref=xin.at[n], send_sem=xs_sem.at[n], recv_sem=xr_sem.at[n],
                                            device_id={'model': lax.rem(stage + 1, stages), 'model2': col}, device_id_type=MESH)

    @pl.when(stage > 0)
    def _():
        for n in range(nx):
            x_send(n).wait_recv()

    def rms_into(src, gain_ref):
        ss = jnp.zeros((n_rows, 1), jnp.float32)
        for n in range(nx):
            v = src[n].astype(jnp.float32)
            ss = ss + jnp.sum(v * v, axis=-1, keepdims=True)
        inv = lax.rsqrt(ss * (1.0 / d_model) + EPS)
        for n in range(nx):
            g = gain_ref[pl.ds(stage, 1), n * BLK:(n + 1) * BLK]
            hbuf[:, n * BLK:(n + 1) * BLK] = (src[n].astype(jnp.float32) * inv * g).astype(jnp.bfloat16)

    rms_into(xin, ga_ref)

    lane = lax.broadcasted_iota(jnp.int32, (n_rows, LANES), 1)
    first_half = lax.rem(lane, head_dim) < head_dim // 2
    low = lane < head_dim

    def rope(y):
        swapped = jnp.where(first_half, pltpu.roll(y, LANES - head_dim // 2, 1), pltpu.roll(y, head_dim // 2, 1))
        return y * cos_ref[...] + swapped * sin_ref[...]

    wait_slot(0)
    wait_slot(1)
    k_all = dot_nn(hbuf[...], ring[0])
    v_all = dot_nn(hbuf[...], ring[1])
    for c in range(kv_heads):
        p = c // 2
        kk = rope(k_all[:, p * LANES:(p + 1) * LANES])
        vv = v_all[:, p * LANES:(p + 1) * LANES]
        if c % 2 == 0:
            packed = jnp.where(low, kk, pltpu.roll(vv, head_dim, 1))
        else:
            packed = jnp.where(low, pltpu.roll(kk, head_dim, 1), vv)
        kvp[c] = packed.astype(jnp.bfloat16)

    def pair_copy():
        return pltpu.make_async_remote_copy(src_ref=kvp.at[:, pl.ds(row_b, seq_b), :], dst_ref=kv_recv, send_sem=pair_sem.at[0], recv_sem=pair_sem.at[1],
                                            device_id={'model': stage, 'model2': col + 1 - 2 * half}, device_id_type=MESH)

    @pl.when(half == 0)
    def _():
        pair_copy().start()

    def q_step(c, carry):
        wait_slot(2 + 2 * c)
        wait_slot(3 + 2 * c)
        h = hbuf[...]
        qs = [dot_nn(h, ring[2 + 2 * c]), dot_nn(h, ring[3 + 2 * c])]
        for t in range(2):
            for p in range(2):
                start = pl.multiple_of((2 * c + t) * BLK + p * LANES, LANES)
                qbuf[:, pl.ds(start, LANES)] = rope(qs[t][:, p * LANES:(p + 1) * LANES]).astype(jnp.bfloat16)
        return carry

    lax.fori_loop(0, nq // 2, q_step, 0)
    for i in range(NSLOT, NSLOT + nq + 2):
        issue(i)

    def kv_copy(d, src_stage, src_col):
        return pltpu.make_async_remote_copy(src_ref=kvp.at[d // (per_head * width)], dst_ref=kv_out.at[src_stage, src_col], send_sem=ks_sem.at[d],
                                            recv_sem=kr_sem.at[src_stage * width + src_col],
                                            device_id={'model': d // width, 'model2': lax.rem(d, width)}, device_id_type=MESH)

    def kv_local():
        return pltpu.make_async_copy(kvp.at[stage // per_head], kv_out.at[stage, col], ks_sem.at[me])

    def kv_start(d, carry):
        @pl.when(d != me)
        def _():
            kv_copy(d, stage, col).start()
        return carry

    lax.fori_loop(0, n_dev, kv_start, 0)
    kv_local().start()

    @pl.when(half == 1)
    def _():
        pair_copy().wait_recv()

    low_s = lax.broadcasted_iota(jnp.int32, (seq_a, LANES), 1) < head_dim
    for c in range(kv_heads):
        own_b = kvp[c, row_b:row_b + seq_b, :]

        @pl.when(half == 0)
        def _():
            kvb[c, 0, 0:seq_b, :] = own_b

        @pl.when(half == 1)
        def _():
            kvb[c, 0, 0:seq_b, :] = kv_recv[c]

        kvb[c, 0, seq_b:2 * seq_b, :] = own_b
        for src, dst in ((kvp[c, 0:seq_a, :], kva), (kvb[c, 0, 0:seq_a, :], kvb)):
            f = src.astype(jnp.float32)
            r = pltpu.roll(f, head_dim, 1)
            dst[c, 1, 0:seq_a, :] = jnp.where(low_s, f, 0.0).astype(jnp.bfloat16)
            dst[c, 1, seq_a:2 * seq_a, :] = jnp.where(low_s, 0.0, r).astype(jnp.bfloat16)
            dst[c, 2, 0:seq_a, :] = jnp.where(low_s, r, 0.0).astype(jnp.bfloat16)
            dst[c, 2, seq_a:2 * seq_a, :] = jnp.where(low_s, 0.0, f).astype(jnp.bfloat16)

    scale = head_dim ** -0.5
    mask_a = mask_a_ref[...] > 0
    mask_b = mask_b_ref[...] > 0
    mask_da = mask_a[seq_a:, :]
    mask_db = mask_b[:n_dec, :]
    low_d = lax.broadcasted_iota(jnp.int32, (n_dec, LANES), 1) < head_dim
    row_d = lax.broadcasted_iota(jnp.int32, (n_dec, LANES), 0)

    def soft(s, mask):
        s = jnp.where(mask, s * scale, NEG)
        m = jnp.max(s, axis=-1, keepdims=True)
        e = jnp.exp(s - m)
        return (e * (1.0 / jnp.sum(e, axis=-1, keepdims=True))).astype(jnp.bfloat16)

    def soft_self(s, mask, s_self):
        s = jnp.where(mask, s * scale, NEG)
        m = jnp.maximum(jnp.max(s, axis=-1, keepdims=True), s_self)
        e = jnp.exp(s - m)
        e_self = jnp.exp(s_self - m)
        inv = 1.0 / (jnp.sum(e, axis=-1, keepdims=True) + e_self)
        return (e * inv).astype(jnp.bfloat16), (e_self * inv).astype(jnp.bfloat16).astype(jnp.float32)

    pairs_per_kv = q_cols // (kv_heads * LANES)
    for c in range(kv_heads):
        kv_d = kvp[c, seq_a:seq_a + n_dec, :].astype(jnp.float32)
        kv_r = pltpu.roll(kv_d, head_dim, 1)
        k_self = jnp.where(low_d, kv_d, kv_r)
        v_self = jnp.where(low_d, kv_r, kv_d)

        def head_pair(t, carry, c=c, k_self=k_self, v_self=v_self):
            hs = pl.ds(pl.multiple_of((c * pairs_per_kv + t) * LANES, LANES), LANES)
            qd = qbuf[seq_a:row_b, hs].astype(jnp.float32)
            prod = qd * k_self
            self_e = jnp.sum(jnp.where(low_d, prod, 0.0), axis=-1, keepdims=True) * scale
            self_o = jnp.sum(jnp.where(low_d, 0.0, prod), axis=-1, keepdims=True) * scale
            s_a = dot_nt(qbuf[0:row_b, hs], kva[c, 1])
            s_b = dot_nt(qbuf[seq_a:n_rows, hs], kvb[c, 1])
            pa = jnp.concatenate([soft(s_a[:seq_a, :seq_a], mask_a[:seq_a]), soft(s_a[:seq_a, seq_a:], mask_a[:seq_a])], axis=1)
            pb = jnp.concatenate([soft(s_b[n_dec:, :seq_a], mask_b[n_dec:]), soft(s_b[n_dec:, seq_a:], mask_b[n_dec:])], axis=1)
            dae, dae_s = soft_self(s_a[seq_a:, :seq_a], mask_da, self_e)
            dao, dao_s = soft_self(s_a[seq_a:, seq_a:], mask_da, self_o)
            dbe, dbe_s = soft_self(s_b[:n_dec, :seq_a], mask_db, self_e)
            dbo, dbo_s = soft_self(s_b[:n_dec, seq_a:], mask_db, self_o)
            o_a = dot_nn(jnp.concatenate([pa, jnp.concatenate([dae, dao], axis=1)], axis=0), kva[c, 2])
            o_b = dot_nn(jnp.concatenate([jnp.concatenate([dbe, dbo], axis=1), pb], axis=0), kvb[c, 2])
            o_da = o_a[seq_a:] + jnp.where(low_d, dae_s, dao_s) * v_self
            o_db = o_b[:n_dec] + jnp.where(low_d, dbe_s, dbo_s) * v_self
            hbuf[0:seq_a, hs] = o_a[:seq_a].astype(jnp.bfloat16)
            hbuf[seq_a:row_b, hs] = jnp.where(row_d == 0, o_da, o_db).astype(jnp.bfloat16)
            hbuf[row_b:n_rows, hs] = o_b[n_dec:].astype(jnp.bfloat16)
            return carry

        lax.fori_loop(0, pairs_per_kv, head_pair, 0)

    def out_step(n, carry):
        s0 = nq + 2 + 2 * n
        wait_slot(s0)
        wait_slot(s0 + 1)
        o = hbuf[...]
        y0 = dot_nn(o, ring[s0])
        y1 = dot_nn(o, ring[s0 + 1])
        x1buf[2 * n] = (xin[2 * n].astype(jnp.float32) + y0).astype(jnp.bfloat16)
        x1buf[2 * n + 1] = (xin[2 * n + 1].astype(jnp.float32) + y1).astype(jnp.bfloat16)
        return carry

    lax.fori_loop(0, nx // 2, out_step, 0)
    for i in range(NSLOT + nq + 2, NSLOT + n_attn):
        issue(i)

    rms_into(x1buf, gm_ref)

    n_tail = len(order) - (NSLOT + n_attn)

    def gu_step(j, carry):
        i0 = n_attn + 2 * j
        sg = lax.rem(i0, NSLOT)
        su = lax.rem(i0 + 1, NSLOT)
        wait_slot(sg)
        wait_slot(su)
        h = hbuf[...]
        g = dot_nn(h, ring[sg])
        u = dot_nn(h, ring[su])
        abuf[j] = (g * (1.0 / (1.0 + jnp.exp(-g))) * u).astype(jnp.bfloat16)

        @pl.when(j < n_tail // 2)
        def _():
            c0 = NSLOT + n_attn - n_up + 2 * j
            ring_copy(cols(w_dt, c0), sg).start()
            ring_copy(cols(w_dt, c0 + 1), su).start()
        return carry

    lax.fori_loop(0, nff, gu_step, 0)

    d_slots = [(n_up + k) % NSLOT for k in range(nff)]
    for s in d_slots:
        wait_slot(s)

    def down_step(n, carry):
        ys = []
        for t in range(2):
            rows = pl.ds(pl.multiple_of((2 * n + t) * BLK, BLK), BLK)
            acc = dot_nt(abuf[0], ring[d_slots[0], rows, :])
            for k in range(1, nff):
                acc = acc + dot_nt(abuf[k], ring[d_slots[k], rows, :])
            ys.append(acc)
        for t in range(2):
            xout[2 * n + t] = (x1buf[2 * n + t].astype(jnp.float32) + ys[t]).astype(jnp.bfloat16)

        @pl.when(stage < stages - 1)
        def _():
            x_send(2 * n).start()
            x_send(2 * n + 1).start()
        return carry

    lax.fori_loop(0, nx // 2, down_step, 0)

    def res_copy(d, src_col):
        return pltpu.make_async_remote_copy(src_ref=res_vm, dst_ref=res_out.at[src_col], send_sem=rs_sem.at[d], recv_sem=rr_sem.at[src_col],
                                            device_id={'model': d // width, 'model2': lax.rem(d, width)}, device_id_type=MESH)

    def res_local():
        return pltpu.make_async_copy(res_vm, res_out.at[col], rs_sem.at[me])

    groups = n_dec // 4
    last = stages - 1

    @pl.when(stage == last)
    def _():
        for j in range(nx // groups):
            acc = dot_nn(sel_ref[0], xout[groups * j])
            for i in range(1, groups):
                acc = acc + dot_nn(sel_ref[i], xout[groups * j + i])
            res_vm[:, j * BLK:(j + 1) * BLK] = acc.astype(jnp.bfloat16)

        def res_start(d, carry):
            @pl.when(d != me)
            def _():
                res_copy(d, col).start()
            return carry

        lax.fori_loop(0, n_dev, res_start, 0)
        res_local().start()

        def res_wait(d, carry):
            @pl.when(d != me)
            def _():
                res_copy(d, col).wait_send()
            return carry

        lax.fori_loop(0, n_dev, res_wait, 0)
        res_local().wait()

    @pl.when(stage < last)
    def _():
        for n in range(nx):
            x_send(n).wait_send()

    @pl.when(half == 0)
    def _():
        pair_copy().wait_send()

    kv_local().wait()

    def kv_wait(d, carry):
        @pl.when(d != me)
        def _():
            kv_copy(d, stage, col).wait_send()
            kv_copy(0, d // width, lax.rem(d, width)).wait_recv()
        return carry

    lax.fori_loop(0, n_dev, kv_wait, 0)

    def res_in(y, carry):
        @pl.when((stage != last) | (y != col))
        def _():
            res_copy(0, y).wait_recv()
        return carry

    lax.fori_loop(0, width, res_in, 0)


def solution(mesh):
    stages = mesh.shape['model']
    width = mesh.shape['model2']
    stage_spec = P('model', None, None)
    in_specs = (P('replica', None, None, None), P('replica', None), P('replica', None),
                stage_spec, stage_spec, stage_spec, stage_spec, P(None, None), P(None, None),
                P(None, None, TP_AXES, None), P(None, None, TP_AXES, None), P(None, None, TP_AXES, None),
                P(None, TP_AXES, None, None), P(None, None, TP_AXES), P(None, None, TP_AXES), P(None, TP_AXES, None))
    cache_spec = P(None, 'replica', None, TP_AXES, None)
    out_specs = (P('replica', None), P('replica', None), cache_spec, cache_spec)

    def shard_body(x_prompt, lengths, x_new, st_qkv, st_out, st_gateup, st_down_t, gain_attn, gain_mlp, tp_query, tp_key, tp_value, tp_out, tp_gate, tp_up, tp_down):
        n_prompts, _, seq_len, d_model = x_prompt.shape
        head_dim = tp_query.shape[-1]
        q_cols = st_out.shape[1]
        kv_heads = (st_qkv.shape[2] - q_cols) // (2 * head_dim)
        ff = st_down_t.shape[2]
        n_dec = 16
        seq_a, seq_b = seq_len, seq_len // 2
        assert n_prompts == width + width // 2 and st_qkv.shape[0] == 1 and tp_key.shape[2] == 1
        n_rows = seq_a + n_dec + seq_b
        groups = n_dec // 4
        col = lax.axis_index('model2')
        half = col % 2
        lens = lengths.reshape(n_prompts)
        ib = width + col // 2
        len_a, len_b = lens[col], lens[ib]
        bf = jnp.bfloat16
        xa, xb = x_new[col], jnp.where(half == 1, x_new[ib], jnp.zeros((d_model,), bf))
        dec_rows = jnp.concatenate([xa[None], xb[None], jnp.zeros((n_dec - 2, d_model), bf)], axis=0)
        ar = jnp.arange(n_rows)
        pos = jnp.where(ar < seq_a, ar, jnp.where(ar == seq_a, len_a, jnp.where(ar == seq_a + 1, len_b, half * seq_b + ar - seq_a - n_dec)))
        cos_t, sin_t = rope_angles(pos, head_dim)
        cos_w = jnp.concatenate([cos_t] * (2 * LANES // head_dim), axis=1)
        sin_w = jnp.concatenate([-sin_t, sin_t] * (LANES // head_dim), axis=1)
        is_dec = (ar >= seq_a) & (ar < seq_a + n_dec)
        key_pos = jnp.arange(seq_len)[None, :]
        seen = is_dec[:, None] | (key_pos <= pos[:, None])
        mask_a = (seen & (key_pos < len_a))[:seq_a + n_dec].astype(jnp.float32)
        mask_b = (seen & (key_pos < len_b))[seq_a:].astype(jnp.float32)
        off_b = len_b - 1 - half * seq_b
        pick = jnp.stack([len_a - 1, jnp.where((off_b >= 0) & (off_b < seq_b), seq_a + n_dec + off_b, -1), jnp.full((), seq_a), jnp.where(half == 1, seq_a + 1, -1)])
        onehot = (pick[:, None] == ar[None, :]).astype(bf)
        eye = jnp.eye(groups, dtype=bf)
        sel = (eye[:, :, None, None] * onehot[None, None]).reshape(groups, n_dec, n_rows)

        dims = (stages, width, kv_heads, head_dim, seq_a, seq_b, n_dec, q_cols, ff)
        nx = d_model // BLK
        n_dev = stages * width
        vmem, hbm = pl.BlockSpec(memory_space=pltpu.VMEM), pl.BlockSpec(memory_space=pl.ANY)
        dma = pltpu.SemaphoreType.DMA
        kv_all, res = pl.pallas_call(
            functools.partial(stage_kernel, dims),
            out_shape=(jax.ShapeDtypeStruct((stages, width, n_rows, LANES), bf), jax.ShapeDtypeStruct((width, n_dec, d_model // groups), bf)),
            in_specs=[hbm, hbm] + [vmem] * 7 + [hbm] * 4,
            out_specs=(hbm, hbm),
            scratch_shapes=[
                pltpu.VMEM((NSLOT, d_model, BLK), bf),
                pltpu.VMEM((nx, n_rows, BLK), bf),
                pltpu.VMEM((nx, n_rows, BLK), bf),
                pltpu.VMEM((n_rows, d_model), bf),
                pltpu.VMEM((n_rows, q_cols), bf),
                pltpu.VMEM((nx, n_rows, BLK), bf),
                pltpu.VMEM((ff // BLK, n_rows, BLK), bf),
                pltpu.VMEM((kv_heads, n_rows, LANES), bf),
                pltpu.VMEM((kv_heads, 3, 2 * seq_a, LANES), bf),
                pltpu.VMEM((kv_heads, 3, 2 * seq_a, LANES), bf),
                pltpu.VMEM((kv_heads, seq_b, LANES), bf),
                pltpu.VMEM((n_dec, d_model // groups), bf),
                dma((NSLOT,)), dma((3 * nx,)), dma((nx,)), dma((nx,)), dma((n_dev,)), dma((n_dev,)), dma((n_dev,)), dma((width,)), dma((2,)),
            ],
            compiler_params=pltpu.CompilerParams(collective_id=0, has_side_effects=True, vmem_limit_bytes=67043328),
        )(x_prompt, dec_rows, cos_w, sin_w, mask_a, mask_b, sel, gain_attn, gain_mlp, st_qkv, st_out, st_gateup, st_down_t)

        picked = res.reshape(width, groups, 4, nx // groups, BLK).transpose(0, 2, 3, 1, 4).reshape(width, 4, d_model)
        last_hidden = jnp.concatenate([picked[:, 0], picked[0::2, 1] + picked[1::2, 1]], axis=0)
        dec_out = jnp.concatenate([picked[:, 2], picked[1::2, 3]], axis=0)

        def cache(part):
            sub = kv_all[..., part * head_dim:(part + 1) * head_dim]
            own = sub[:, :, :seq_a + 1]
            lo, hi = sub[:, 0::2, seq_a + n_dec:], sub[:, 1::2, seq_a + n_dec:]
            shared = jnp.concatenate([lo, hi, sub[:, 1::2, seq_a + 1:seq_a + 2]], axis=2)
            return jnp.concatenate([own, shared], axis=1)[:, :, :, None, :]

        return dec_out, last_hidden, cache(0), cache(1)

    return jax.shard_map(shard_body, mesh=mesh, in_specs=in_specs, out_specs=out_specs, check_vma=False)
```

time: 1670 us -> 393 us (0.24)
  blocking collectives: 744 us -> 0 us
  matrix products: 652 us -> 0 us
  Pallas kernels: 0 us -> 367 us
  other arithmetic: 79.1 us -> 9.76 us
  starting transfers between devices: 68.4 us -> 0 us
  waiting for transfers between devices: 46.2 us -> 0 us
  loops' own time: 33.8 us -> 0 us
  local copies, waits for them, and re-layouts: 38.8 us -> 13.6 us
    psum x17 -> x0, blocking collectives: 744 us -> none  [the longest x8 361 us: layer_fn(): lax.psum(jnp.einsum('bhe,hed->bd', attn_out, w_outp, preferred_element_ty...]
    dot_general x142 -> x0, matrix products: 652 us -> none  [the longest x13 260 us: stage_layer(): jnp.einsum('bsd,df->bsf', normed_mlp, w_gateup, preferred_element_type=jn...]
    pallas_call x0 -> x1, Pallas kernels: none -> 367 us  [shard_body(): pl.pallas_call(functools.partial(stage_kernel, dims), out_shape=(jax.Shap...]
    ppermute x13 -> x0, starting transfers between devices: 57.7 us -> none  [tick_fn(): recv_act = lax.ppermute(hidden_x, 'model', send_pairs)]
    ppermute x13 -> x0, waiting for transfers between devices: 34.3 us -> none  [tick_fn(): recv_act = lax.ppermute(hidden_x, 'model', send_pairs)]
    another operation x2 -> x0, loops' own time: 33.8 us -> none  [the longest x1 33.4 us: shard_body(): lax.scan(tick_fn, init_carry, jnp.arange(num_micro + stages - 1))[0]]
    reduce_sum x50 -> x0, other arithmetic: 25.8 us -> none  [the longest x29 19.2 us: rms_norm(): inv_rms = lax.rsqrt(jnp.mean(x_f32 * x_f32, axis=-1, keepdims=True) + EPS)]
    dynamic_slice x30 -> x1, local copies, waits for them, and re-layouts: 23.1 us -> 1.32 us  [shard_body(): len_a, len_b = (lens[col], lens[ib])]
  transfers between devices with their start and end apart: 15 -> 0, of which waited for: 14 -> 0; matrix products, arithmetic and copies ran while one was open for 1% -> 0% of each run, Pallas kernels for 0% -> 0%
where the time goes in v1:
time: 393 us
  Pallas kernels  367 us (93%)
  local copies, waits for them, and re-layouts  13.6 us (3%)
  other arithmetic  9.76 us (2%)
    pallas_call x1, Pallas kernels, shard_body(): pl.pallas_call(functools.partial(stage_kernel, dims), out_shape=(jax.Shap...  367 us

profile of v1, /device:TPU:97, one launch (start us, length us, event | category | flops | bytes accessed | tf_op | source)
XLA Modules:
  0.0 392.7 jit_solution(2173261942680634790)
XLA Ops:
  0.7 0.9 constant_dynamic-slice_fusion.2
  1.5 0.1 pad.26.clone
  1.6 0.7 maximum_maximum_fusion.dec_hbm
  2.3 1.3 constant_dynamic-slice_fusion.1
  3.6 1.3 fusion.6
  5.0 0.4 fusion.3
  5.4 0.9 pad_maximum_fusion
  6.3 0.1 fusion
  6.5 0.7 iota_compare_fusion.4
  7.1 0.6 fusion.1.mask_a_ref
  7.8 0.6 iota_compare_fusion.3
  8.4 0.6 fusion.2.mask_b_ref
  10.4 0.1 pad_add_fusion
  10.4 0.1 fusion.4
  10.5 0.1 mul.55
  10.6 0.1 mul.56
  10.7 0.7 broadcast_multiply_fusion.sel_ref
  11.4 367.2 %shard_map.120 = (bf16[8,4,208,128]{3,2,1,0:T(8,128)(2,1)}, bf16[4,16,512]{2,1,0:T(8,128)(2,1)}) custom-call(bf16[6,1,128,2048]{3,2,1,0:T(8,128)(2,1)} %x_hbm.1, bf16[16,2048]{1,0:T(8,128)(2,1)} %maximum_maximum_fusion.dec_hbm, f32[208,128]{1,0:T(8,128)} %get-tuple-element.35.cos_ref, f32[208,128]{1,0:T(8,128)} %get-tuple-element.36.sin_ref, ...), custom_call_target="tpu_custom_call" | custom-call | tf_op jit(solution)/shard_map/pallas_call | solution.py:440
  378.6 0.9 reshape.90
  379.6 0.6 pad_maximum_fusion.2
  380.4 0.6 pad_maximum_fusion.3
  381.0 0.0 copy-start
  381.0 4.0 %fusion.9 = (bf16[8,4,208,64]{3,2,1,0:T(8,128)(2,1)}, bf16[8,4,208,64]{3,2,1,0:T(8,128)(2,1)S(1)}) fusion(bf16[8,4,208,128]{3,2,1,0:T(8,128)(2,1)} %get-tuple-element.7), kind=kLoop, calls=%fused_computation.39 | loop fusion | bytes 3407872 | tf_op jit(solution)/shard_map/slice | solution.py:468
  385.0 0.1 fusion.10
  385.1 0.0 copy-done
  385.1 0.4 fusion.7
  385.5 0.3 maximum_bitcast_fusion
  385.8 2.3 copy.18
  388.2 0.8 slice.69
  388.9 1.1 fusion.8
  390.0 0.3 maximum_bitcast_fusion.1
  390.4 2.3 copy.19
  (14 shorter events, 0.3 us)
Async XLA Ops:
  381.0 4.1 %copy-start = (bf16[8,4,208,128]{3,2,1,0:T(8,128)(2,1)S(1)}, bf16[8,4,208,128]{3,2,1,0:T(8,128)(2,1)}, u32[]{:S(2)}) copy-start(bf16[8,4,208,128]{3,2,1,0:T(8,128)(2,1)} %get-tuple-element.7) | copy-start | bytes 5111812

commit v2 on v1

v2 whole, which is shorter than its diff:
```python
import functools

import jax
import jax.numpy as jnp
import numpy as np
from jax import lax
from jax.experimental import pallas as pl
from jax.experimental.pallas import tpu as pltpu
from jax.sharding import PartitionSpec as P

EPS = 1e-5
THETA = 10000.0
TP_AXES = ('model', 'model2')
MESH = pl.DeviceIdType.MESH
BLK = 256
LANES = 128
NSLOT = 50
NEG = -1e30
QU = 4
GU = 4


def rope_table(count, head_dim):
    half_dim = head_dim // 2
    inv_freq = np.power(np.float32(THETA), np.arange(half_dim, dtype=np.float32) * np.float32(-2.0 / head_dim))
    angles = (np.arange(count, dtype=np.float32)[:, None] * inv_freq.astype(np.float32)).astype(np.float64)
    cos, sin = np.cos(angles).astype(np.float32), np.sin(angles).astype(np.float32)
    return jnp.asarray(np.tile(cos, (1, 2 * LANES // head_dim))), jnp.asarray(np.tile(np.concatenate([-sin, sin], axis=1), (1, LANES // head_dim)))


def dot_nn(a, b):
    return lax.dot_general(a, b, (((1,), (0,)), ((), ())), preferred_element_type=jnp.float32)


def dot_nt(a, b):
    return lax.dot_general(a, b, (((1,), (1,)), ((), ())), preferred_element_type=jnp.float32)


def cat(ref, first, count):
    return jnp.concatenate([ref[first + t] for t in range(count)], axis=1)


def stage_kernel(dims, lens_ref, cos_t, sin_t, ga_ref, gm_ref, new_ref, x_hbm, w_qkv, w_out, w_gu, w_dt, kv_out, dec_out, res_out,
                 ring, xin, xout, hbuf, qbuf, x1buf, abuf, kvp, kva, kvb, kv_recv, kvt, cosv, sinv, gains, mask_a, mask_b, res_vm, small, asmall, tsmall,
                 ring_sem, x0_sem, xs_sem, xr_sem, ks_sem, kr_sem, kd_sem, rs_sem, rr_sem, pair_sem):
    stages, width, kv_heads, head_dim, seq_a, seq_b, n_dec, q_cols, ff, n_prompts = dims
    n_rows = seq_a + n_dec + seq_b
    row_b = seq_a + n_dec
    d_model = w_out.shape[2]
    nx = d_model // BLK
    nl = d_model // LANES
    nq = q_cols // BLK
    nff = ff // BLK
    n_dev = stages * width
    per_head = stages // kv_heads
    last = stages - 1
    bf, f32 = jnp.bfloat16, jnp.float32
    stage = lax.axis_index('model')
    col = lax.axis_index('model2')
    me = stage * width + col
    half = lax.rem(col, 2)
    shared = width + col // 2
    len_a = lens_ref[col, 0]
    len_b = lens_ref[shared, 0]

    def ring_copy(ref, c, slot, t):
        start = pl.multiple_of(c * BLK + t * LANES, LANES)
        return pltpu.make_async_copy(ref.at[0, :, pl.ds(start, LANES)], ring.at[2 * slot + t], ring_sem.at[2 * slot + t])

    def ring_start(ref, c, slot):
        ring_copy(ref, c, slot, 0).start()
        ring_copy(ref, c, slot, 1).start()

    def wait_slot(slot):
        ring_copy(w_out, 0, slot, 0).wait()
        ring_copy(w_out, 0, slot, 1).wait()

    def weight(slot):
        return cat(ring, 2 * slot, 2)

    order = [(w_qkv, nq), (w_qkv, nq + 1)] + [(w_qkv, c) for c in range(nq)] + [(w_out, c) for c in range(nx)]
    n_attn = len(order)
    for j in range(nff):
        order += [(w_gu, j), (w_gu, nff + j)]
    n_up = len(order)
    order += [(w_dt, c) for c in range(nff)]

    def issue(i):
        ref, c = order[i]
        ring_start(ref, c, i % NSLOT)

    def x0_copies():
        out = []
        for n in range(nl):
            cs = pl.ds(n * LANES, LANES)
            out.append(pltpu.make_async_copy(x_hbm.at[col, 0, :, cs], xin.at[n, pl.ds(0, seq_a), :], x0_sem.at[2 * n]))
            out.append(pltpu.make_async_copy(x_hbm.at[shared, 0, pl.ds(pl.multiple_of(half * seq_b, seq_b), seq_b), cs], xin.at[n, pl.ds(row_b, seq_b), :], x0_sem.at[2 * n + 1]))
        return out

    @pl.when(stage == 0)
    def _():
        for c in x0_copies():
            c.start()

    for i in range(NSLOT):
        issue(i)

    barrier = pltpu.get_barrier_semaphore()

    def device(d):
        return {'model': d // width, 'model2': lax.rem(d, width)}

    def greet(i, carry):
        pl.semaphore_signal(barrier, inc=1, device_id=device(lax.rem(me + i, n_dev)), device_id_type=MESH)
        return carry

    lax.fori_loop(1, n_dev, greet, 0)

    for which, ref in ((0, ga_ref), (1, gm_ref)):
        mine = lax.broadcasted_iota(jnp.int32, (ref.shape[0], LANES), 0) == stage
        for n in range(nl):
            gains[which, n, 0:1, :] = jnp.sum(jnp.where(mine, ref[:, n * LANES:(n + 1) * LANES], 0.0), axis=0, keepdims=True)
    row_d = lax.broadcasted_iota(jnp.int32, (n_dec, LANES), 0)
    for table, out in ((cos_t, cosv), (sin_t, sinv)):
        out[0:seq_a, :] = table[0:seq_a, :]
        out[seq_a:row_b, :] = jnp.where(row_d == 0, table[pl.ds(len_a, 1), :], table[pl.ds(len_b, 1), :])
        out[row_b:n_rows, :] = table[pl.ds(pl.multiple_of(half * seq_b, seq_b), seq_b), :]

    for table, out in ((cos_t, 0), (sin_t, 1)):
        picked = jnp.where(row_d == 0, table[pl.ds(jnp.maximum(len_a - 1, 0), 1), :], table[pl.ds(jnp.maximum(len_b - 1, 0), 1), :])
        picked = jnp.where(row_d == 2, table[pl.ds(len_a, 1), :], picked)
        tsmall[out] = jnp.where(row_d == 3, table[pl.ds(len_b, 1), :], picked)

    def fill_mask(out, rows, offset, length):
        key = lax.broadcasted_iota(jnp.int32, (rows, LANES), 1)
        row = lax.broadcasted_iota(jnp.int32, (rows, LANES), 0) + offset
        return ((key <= row) & (key < length)).astype(f32)

    key_d = lax.broadcasted_iota(jnp.int32, (n_dec, LANES), 1)
    mask_a[0:seq_a, :] = fill_mask(mask_a, seq_a, 0, len_a)
    mask_a[seq_a:row_b, :] = (key_d < len_a).astype(f32)
    mask_b[0:n_dec, :] = (key_d < len_b).astype(f32)
    mask_b[n_dec:n_dec + seq_b, :] = fill_mask(mask_b, seq_b, half * seq_b, len_b)

    @pl.when(stage == 0)
    def _():
        for n in range(nl):
            acc = jnp.zeros((n_dec, LANES), f32)
            for b in range(n_prompts):
                take = ((row_d == 0) & (col == b)) | ((row_d == 1) & (half == 1) & (shared == b))
                acc = acc + jnp.where(take, new_ref[b:b + 1, n * LANES:(n + 1) * LANES].astype(f32), 0.0)
            xin[n, seq_a:row_b, :] = acc.astype(bf)
        for c in x0_copies():
            c.wait()

    def x_send(n):
        two = pl.ds(2 * n, 2)
        return pltpu.make_async_remote_copy(src_ref=xout.at[two], dst_ref=xin.at[two], send_sem=xs_sem.at[n], recv_sem=xr_sem.at[n],
                                            device_id={'model': lax.rem(stage + 1, stages), 'model2': col}, device_id_type=MESH)

    @pl.when(stage > 0)
    def _():
        for n in range(nx):
            x_send(n).wait_recv()

    def rms_into(src, which, dst):
        ss = jnp.zeros(src.shape[1:], f32)
        for n in range(nl):
            v = src[n].astype(f32)
            ss = ss + v * v
        inv = lax.rsqrt(jnp.sum(ss, axis=-1, keepdims=True) * (1.0 / d_model) + EPS)
        for n in range(nl):
            dst[n] = (src[n].astype(f32) * inv * gains[which, n, 0:1, :]).astype(bf)

    rms_into(xin, 0, hbuf)

    low = lax.broadcasted_iota(jnp.int32, (n_rows, LANES), 1) < head_dim

    def rope(y, cos, sin):
        lane = lax.broadcasted_iota(jnp.int32, y.shape, 1)
        first_half = lax.rem(lane, head_dim) < head_dim // 2
        swapped = jnp.where(first_half, pltpu.roll(y, LANES - head_dim // 2, 1), pltpu.roll(y, head_dim // 2, 1))
        return y * cos + swapped * sin

    wait_slot(0)
    wait_slot(1)
    h = cat(hbuf, 0, nl)
    k_all = dot_nn(h, weight(0))
    v_all = dot_nn(h, weight(1))
    for c in range(kv_heads):
        p = c // 2
        kk = rope(k_all[:, p * LANES:(p + 1) * LANES], cosv[...], sinv[...])
        vv = v_all[:, p * LANES:(p + 1) * LANES]
        if c % 2 == 0:
            packed = jnp.where(low, kk, pltpu.roll(vv, head_dim, 1))
        else:
            packed = jnp.where(low, pltpu.roll(kk, head_dim, 1), vv)
        kvp[c] = packed.astype(bf)

    pl.semaphore_wait(barrier, n_dev - 1)

    def pair_copy():
        return pltpu.make_async_remote_copy(src_ref=kvp.at[:, pl.ds(row_b, seq_b), :], dst_ref=kv_recv, send_sem=pair_sem.at[0], recv_sem=pair_sem.at[1],
                                            device_id={'model': stage, 'model2': col + 1 - 2 * half}, device_id_type=MESH)

    @pl.when(half == 0)
    def _():
        pair_copy().start()

    def queries(src, dst, cos, sin):
        def q_step(it, carry):
            for r in range(QU):
                wait_slot(2 + QU * it + r)
            h = cat(src, 0, nl)
            qs = [dot_nn(h, weight(2 + QU * it + r)) for r in range(QU)]
            for r in range(QU):
                for p in range(2):
                    dst[2 * (QU * it + r) + p] = rope(qs[r][:, p * LANES:(p + 1) * LANES], cos[...], sin[...]).astype(bf)
            return carry

        lax.fori_loop(0, nq // QU, q_step, 0)

    @pl.when(stage < last)
    def _():
        queries(hbuf, qbuf, cosv, sinv)
        for i in range(NSLOT, NSLOT + nq + 2):
            issue(i)

    @pl.when(half == 1)
    def _():
        pair_copy().wait_recv()

    low_s = lax.broadcasted_iota(jnp.int32, (seq_a, LANES), 1) < head_dim
    for c in range(kv_heads):
        own_b = kvp[c, row_b:row_b + seq_b, :]

        @pl.when(half == 0)
        def _():
            kvb[c, 2, 0:seq_b, :] = own_b

        @pl.when(half == 1)
        def _():
            kvb[c, 2, 0:seq_b, :] = kv_recv[c]

        kvb[c, 2, seq_b:2 * seq_b, :] = own_b
        for src, dst in ((kvp[c, 0:seq_a, :], kva), (kvb[c, 2, 0:seq_a, :], kvb)):
            f = src.astype(f32)
            r = pltpu.roll(f, head_dim, 1)
            dst[c, 0, 0:seq_a, :] = jnp.where(low_s, f, 0.0).astype(bf)
            dst[c, 0, seq_a:2 * seq_a, :] = jnp.where(low_s, 0.0, r).astype(bf)
            dst[c, 1, 0:seq_a, :] = jnp.where(low_s, r, 0.0).astype(bf)
            dst[c, 1, seq_a:2 * seq_a, :] = jnp.where(low_s, 0.0, f).astype(bf)

    def kv_copy(d, which, src_stage, prompt):
        return pltpu.make_async_remote_copy(src_ref=kvt.at[d // (per_head * width), which], dst_ref=kv_out.at[src_stage, prompt], send_sem=ks_sem.at[which, d],
                                            recv_sem=kr_sem.at[src_stage * n_prompts + prompt], device_id=device(d), device_id_type=MESH)

    def kv_local(which, prompt):
        return pltpu.make_async_copy(kvt.at[stage // per_head, which], kv_out.at[stage, prompt], ks_sem.at[which, me])

    own_rows = pl.ds(seq_a, n_dec)

    def dec_copy(d, src_stage, src_col):
        return pltpu.make_async_remote_copy(src_ref=kvp.at[d // (per_head * width), own_rows], dst_ref=dec_out.at[src_stage, src_col], send_sem=ks_sem.at[2, d],
                                            recv_sem=kd_sem.at[src_stage * width + src_col], device_id=device(d), device_id_type=MESH)

    def dec_local():
        return pltpu.make_async_copy(kvp.at[stage // per_head, own_rows], dec_out.at[stage, col], ks_sem.at[2, me])

    def kv_fill(which, src):
        for c in range(kv_heads):
            t = src(c).astype(f32).T
            for part in range(2):
                kvt[c, which, part] = t[part * head_dim:(part + 1) * head_dim].astype(bf)

    def others(step):
        def body(i, carry):
            step(lax.rem(me + i, n_dev))
            return carry

        lax.fori_loop(1, n_dev, body, 0)

    def kv_emit():
        others(lambda d: dec_copy(d, stage, col).start())
        dec_local().start()
        kv_fill(0, lambda c: kvp[c, 0:seq_a, :])
        others(lambda d: kv_copy(d, 0, stage, col).start())
        kv_local(0, col).start()

        @pl.when(half == 1)
        def _():
            kv_fill(1, lambda c: kvb[c, 2, 0:seq_a, :])
            others(lambda d: kv_copy(d, 1, stage, shared).start())
            kv_local(1, shared).start()

    scale = head_dim ** -0.5
    low_d = lax.broadcasted_iota(jnp.int32, (n_dec, LANES), 1) < head_dim

    def soft(s, mask):
        s = jnp.where(mask > 0, s * scale, NEG)
        m = jnp.max(s, axis=-1, keepdims=True)
        e = jnp.exp(s - m)
        return (e * (1.0 / jnp.sum(e, axis=-1, keepdims=True))).astype(bf)

    def soft_self(s, mask, s_self):
        s = jnp.where(mask > 0, s * scale, NEG)
        m = jnp.maximum(jnp.max(s, axis=-1, keepdims=True), s_self)
        e = jnp.exp(s - m)
        e_self = jnp.exp(s_self - m)
        inv = 1.0 / (jnp.sum(e, axis=-1, keepdims=True) + e_self)
        return (e * inv).astype(bf), (e_self * inv).astype(bf).astype(f32)

    pairs_per_kv = q_cols // (kv_heads * LANES)

    def kv_head(c, carry):
        kv_d = kvp[c, seq_a:row_b, :].astype(f32)
        kv_r = pltpu.roll(kv_d, head_dim, 1)
        k_self = jnp.where(low_d, kv_d, kv_r)
        v_self = jnp.where(low_d, kv_r, kv_d)
        for t in range(pairs_per_kv):
            hp = c * pairs_per_kv + t
            prod = qbuf[hp, seq_a:row_b, :].astype(f32) * k_self
            self_e = jnp.sum(jnp.where(low_d, prod, 0.0), axis=-1, keepdims=True) * scale
            self_o = jnp.sum(jnp.where(low_d, 0.0, prod), axis=-1, keepdims=True) * scale
            s_a = dot_nt(qbuf[hp, 0:row_b, :], kva[c, 0])
            s_b = dot_nt(qbuf[hp, seq_a:n_rows, :], kvb[c, 0])
            ma, mda = mask_a[0:seq_a, :], mask_a[seq_a:row_b, :]
            mdb, mb = mask_b[0:n_dec, :], mask_b[n_dec:n_dec + seq_b, :]
            pa = jnp.concatenate([soft(s_a[:seq_a, :seq_a], ma), soft(s_a[:seq_a, seq_a:], ma)], axis=1)
            pb = jnp.concatenate([soft(s_b[n_dec:, :seq_a], mb), soft(s_b[n_dec:, seq_a:], mb)], axis=1)
            dae, dae_s = soft_self(s_a[seq_a:, :seq_a], mda, self_e)
            dao, dao_s = soft_self(s_a[seq_a:, seq_a:], mda, self_o)
            dbe, dbe_s = soft_self(s_b[:n_dec, :seq_a], mdb, self_e)
            dbo, dbo_s = soft_self(s_b[:n_dec, seq_a:], mdb, self_o)
            o_a = dot_nn(jnp.concatenate([pa, jnp.concatenate([dae, dao], axis=1)], axis=0), kva[c, 1])
            o_b = dot_nn(jnp.concatenate([jnp.concatenate([dbe, dbo], axis=1), pb], axis=0), kvb[c, 1])
            o_da = o_a[seq_a:] + jnp.where(low_d, dae_s, dao_s) * v_self
            o_db = o_b[:n_dec] + jnp.where(low_d, dbe_s, dbo_s) * v_self
            hbuf[hp, 0:seq_a, :] = o_a[:seq_a].astype(bf)
            hbuf[hp, seq_a:row_b, :] = jnp.where(row_d == 0, o_da, o_db).astype(bf)
            hbuf[hp, row_b:n_rows, :] = o_b[n_dec:].astype(bf)
        return carry

    def project(src, res, dst):
        def out_step(it, carry):
            s0 = nq + 2 + QU * it
            for r in range(QU):
                wait_slot(s0 + r)
            o = cat(src, 0, nl)
            ys = [dot_nn(o, weight(s0 + r)) for r in range(QU)]
            for r in range(QU):
                for p in range(2):
                    n = 2 * (QU * it + r) + p
                    dst[n] = (res[n].astype(f32) + ys[r][:, p * LANES:(p + 1) * LANES]).astype(bf)
            return carry

        lax.fori_loop(0, nx // QU, out_step, 0)
        for i in range(NSLOT + nq + 2, NSLOT + n_attn):
            issue(i)

    n_loop = (NSLOT - n_attn) // 2 // GU * GU
    n_down = (len(order) - NSLOT - n_attn) // 2

    def gate_up(src, dst):
        def some(pairs):
            for j, sg in pairs:
                wait_slot(sg)
                wait_slot(sg + 1)
            h = cat(src, 0, nl)
            for j, sg in pairs:
                g = dot_nn(h, weight(sg))
                u = dot_nn(h, weight(sg + 1))
                a = (g * (1.0 / (1.0 + jnp.exp(-g))) * u).astype(bf)
                dst[2 * j] = a[:, :LANES]
                dst[2 * j + 1] = a[:, LANES:]

        def gu_step(it, carry):
            some([(GU * it + r, n_attn + 2 * (GU * it + r)) for r in range(GU)])

            @pl.when(it < n_down // GU)
            def _():
                for r in range(2 * GU):
                    ring_start(w_dt, NSLOT + n_attn - n_up + 2 * GU * it + r, n_attn + 2 * GU * it + r)
            return carry

        lax.fori_loop(0, n_loop // GU, gu_step, 0)
        some([(j, (n_attn + 2 * j) % NSLOT) for j in range(n_loop, nff)])

    d_slots = [(n_up + k) % NSLOT for k in range(nff)]

    def down(src, res, dst, send):
        for s in d_slots:
            wait_slot(s)

        def down_step(n, carry):
            ys = []
            for t in range(2):
                rows = pl.ds(pl.multiple_of((2 * n + t) * BLK, BLK), BLK)
                acc = None
                for k in range(nff):
                    w = jnp.concatenate([ring[2 * d_slots[k], rows, :], ring[2 * d_slots[k] + 1, rows, :]], axis=1)
                    y = dot_nt(cat(src, 2 * k, 2), w)
                    acc = y if acc is None else acc + y
                ys.append(acc)
            for t in range(2):
                for p in range(2):
                    i = 2 * (2 * n + t) + p
                    dst[i] = (res[i].astype(f32) + ys[t][:, p * LANES:(p + 1) * LANES]).astype(bf)
            if send:
                x_send(2 * n).start()
                x_send(2 * n + 1).start()
            return carry

        lax.fori_loop(0, nx // 2, down_step, 0)

    @pl.when(stage < last)
    def _():
        lax.fori_loop(0, kv_heads, kv_head, 0)
        project(hbuf, xin, x1buf)
        rms_into(x1buf, 1, hbuf)
        gate_up(hbuf, abuf)
        down(abuf, x1buf, xout, True)
        kv_emit()

    def res_copy(d, src_col):
        return pltpu.make_async_remote_copy(src_ref=res_vm, dst_ref=res_out.at[src_col], send_sem=rs_sem.at[d], recv_sem=rr_sem.at[src_col],
                                            device_id=device(d), device_id_type=MESH)

    def res_local():
        return pltpu.make_async_copy(res_vm, res_out.at[col], rs_sem.at[me])

    groups = n_dec // 4

    @pl.when(stage == last)
    def _():
        xs, hs, qs, x1s, ys = (small.at[i] for i in range(5))
        who = lax.broadcasted_iota(jnp.int32, (n_dec, n_rows), 0)
        at = lax.broadcasted_iota(jnp.int32, (n_dec, n_rows), 1)
        off_b = len_b - 1 - half * seq_b
        hit = ((who == 0) & (at == len_a - 1)) | ((who == 1) & (at >= row_b) & (at == row_b + off_b)) | ((who == 2) & (at == seq_a)) | ((who == 3) & (half == 1) & (at == seq_a + 1))
        sel = jnp.where(hit, 1.0, 0.0).astype(bf)
        for n in range(nl // 2):
            for src, dst in ((xin, xs), (hbuf, hs)):
                y = dot_nn(sel, cat(src, 2 * n, 2)).astype(bf)
                dst[2 * n] = y[:, :LANES]
                dst[2 * n + 1] = y[:, LANES:]
        queries(hs, qs, tsmall.at[0], tsmall.at[1])
        for i in range(NSLOT, NSLOT + nq + 2):
            issue(i)
        kv_emit()

        stack = pairs_per_kv * n_dec
        key = lax.broadcasted_iota(jnp.int32, (stack, LANES), 1)
        row = lax.rem(lax.broadcasted_iota(jnp.int32, (stack, LANES), 0), n_dec)
        low_k = key < head_dim
        mk_a, mk_b = (key < len_a).astype(f32), (key < len_b).astype(f32)
        decode = (row[:, 0:1] == 2) | (row[:, 0:1] == 3)
        from_a = lax.rem(row, 2) == 0
        for c in range(kv_heads):
            kd = kvp[c, seq_a:row_b, :].astype(f32)
            kr = pltpu.roll(kd, head_dim, 1)
            k_two, v_two = jnp.where(low_d, kd, kr), jnp.where(low_d, kr, kd)
            k_self = jnp.where(from_a, k_two[0:1], k_two[1:2])
            v_self = jnp.where(from_a, v_two[0:1], v_two[1:2])
            q4 = jnp.concatenate([qs[c * pairs_per_kv + t] for t in range(pairs_per_kv)], axis=0)
            prod = q4.astype(f32) * k_self
            self_e = jnp.where(decode, jnp.sum(jnp.where(low_k, prod, 0.0), axis=-1, keepdims=True) * scale, NEG)
            self_o = jnp.where(decode, jnp.sum(jnp.where(low_k, 0.0, prod), axis=-1, keepdims=True) * scale, NEG)
            outs = []
            for kv, mk in ((kva, mk_a), (kvb, mk_b)):
                sc = dot_nt(q4, kv[c, 0])
                pe, pe_s = soft_self(sc[:, :seq_a], mk, self_e)
                po, po_s = soft_self(sc[:, seq_a:], mk, self_o)
                outs.append(dot_nn(jnp.concatenate([pe, po], axis=1), kv[c, 1]) + jnp.where(low_k, pe_s, po_s) * v_self)
            o = jnp.where(from_a, outs[0], outs[1]).astype(bf)
            for t in range(pairs_per_kv):
                hs[c * pairs_per_kv + t] = o[t * n_dec:(t + 1) * n_dec]

        project(hs, xs, x1s)
        rms_into(x1s, 1, hs)
        gate_up(hs, asmall)
        down(asmall, x1s, ys, False)
        keep = (row_d == 0) | (row_d == 2) | ((row_d == 1) & (off_b >= 0) & (off_b < seq_b)) | ((row_d == 3) & (half == 1))
        for n in range(2 * nx // groups):
            j, p = n // 2, n % 2
            acc = jnp.zeros((n_dec, LANES), f32)
            for i in range(groups):
                y = jnp.where(keep, ys[2 * (groups * j + i) + p].astype(f32), 0.0)
                y = pltpu.roll(y, 4 * i, 0) if i else y
                acc = jnp.where(row_d // 4 == i, y, acc)
            res_vm[:, n * LANES:(n + 1) * LANES] = acc.astype(bf)
        others(lambda d: res_copy(d, col).start())
        res_local().start()
        others(lambda d: res_copy(d, col).wait_send())
        res_local().wait()

    @pl.when(stage < last)
    def _():
        for n in range(nx):
            x_send(n).wait_send()

    @pl.when(half == 0)
    def _():
        pair_copy().wait_send()

    others(lambda d: dec_copy(d, stage, col).wait_send())
    dec_local().wait()
    others(lambda d: kv_copy(d, 0, stage, col).wait_send())
    kv_local(0, col).wait()

    @pl.when(half == 1)
    def _():
        others(lambda d: kv_copy(d, 1, stage, shared).wait_send())
        kv_local(1, shared).wait()

    others(lambda d: dec_copy(0, d // width, lax.rem(d, width)).wait_recv())
    for b in range(n_prompts):
        owner = b if b < width else 2 * (b - width) + 1

        def kv_in(s, carry, b=b, owner=owner):
            @pl.when((s != stage) | (col != owner))
            def _():
                kv_copy(0, 0, s, b).wait_recv()
            return carry

        lax.fori_loop(0, stages, kv_in, 0)

    def res_in(y, carry):
        @pl.when((stage != last) | (y != col))
        def _():
            res_copy(0, y).wait_recv()
        return carry

    lax.fori_loop(0, width, res_in, 0)


def solution(mesh):
    stages = mesh.shape['model']
    width = mesh.shape['model2']
    stage_spec = P('model', None, None)
    in_specs = (P('replica', None, None, None), P('replica', None), P('replica', None),
                stage_spec, stage_spec, stage_spec, stage_spec, P(None, None), P(None, None),
                P(None, None, TP_AXES, None), P(None, None, TP_AXES, None), P(None, None, TP_AXES, None),
                P(None, TP_AXES, None, None), P(None, None, TP_AXES), P(None, None, TP_AXES), P(None, TP_AXES, None))
    cache_spec = P(None, 'replica', None, TP_AXES, None)
    out_specs = (P('replica', None), P('replica', None), cache_spec, cache_spec)

    def shard_body(x_prompt, lengths, x_new, st_qkv, st_out, st_gateup, st_down_t, gain_attn, gain_mlp, tp_query, tp_key, tp_value, tp_out, tp_gate, tp_up, tp_down):
        n_prompts, _, seq_len, d_model = x_prompt.shape
        head_dim = tp_query.shape[-1]
        q_cols = st_out.shape[1]
        kv_heads = (st_qkv.shape[2] - q_cols) // (2 * head_dim)
        ff = st_down_t.shape[2]
        n_dec = 16
        seq_a, seq_b = seq_len, seq_len // 2
        assert n_prompts == width + width // 2 and st_qkv.shape[0] == 1 and tp_key.shape[2] == 1
        n_rows = seq_a + n_dec + seq_b
        groups = n_dec // 4
        bf, f32 = jnp.bfloat16, jnp.float32
        cos_t, sin_t = rope_table(seq_len + 8, head_dim)
        dims = (stages, width, kv_heads, head_dim, seq_a, seq_b, n_dec, q_cols, ff, n_prompts)
        nx, nl = d_model // BLK, d_model // LANES
        n_dev = stages * width
        vmem, hbm = pl.BlockSpec(memory_space=pltpu.VMEM), pl.BlockSpec(memory_space=pl.ANY)
        smem = pl.BlockSpec(memory_space=pltpu.SMEM)
        dma = pltpu.SemaphoreType.DMA
        kv_all, dec_all, res = pl.pallas_call(
            functools.partial(stage_kernel, dims),
            out_shape=(jax.ShapeDtypeStruct((stages, n_prompts, 2, head_dim, seq_len), bf), jax.ShapeDtypeStruct((stages, width, n_dec, LANES), bf), jax.ShapeDtypeStruct((width, n_dec, d_model // groups), bf)),
            in_specs=[smem] + [vmem] * 5 + [hbm] * 5,
            out_specs=(hbm, hbm, hbm),
            scratch_shapes=[
                pltpu.VMEM((2 * NSLOT, d_model, LANES), bf),
                pltpu.VMEM((nl, n_rows, LANES), bf),
                pltpu.VMEM((nl, n_rows, LANES), bf),
                pltpu.VMEM((nl, n_rows, LANES), bf),
                pltpu.VMEM((q_cols // LANES, n_rows, LANES), bf),
                pltpu.VMEM((nl, n_rows, LANES), bf),
                pltpu.VMEM((ff // LANES, n_rows, LANES), bf),
                pltpu.VMEM((kv_heads, n_rows, LANES), bf),
                pltpu.VMEM((kv_heads, 2, 2 * seq_a, LANES), bf),
                pltpu.VMEM((kv_heads, 3, 2 * seq_a, LANES), bf),
                pltpu.VMEM((kv_heads, seq_b, LANES), bf),
                pltpu.VMEM((kv_heads, 2, 2, head_dim, seq_len), bf),
                pltpu.VMEM((n_rows, LANES), f32),
                pltpu.VMEM((n_rows, LANES), f32),
                pltpu.VMEM((2, nl, 8, LANES), f32),
                pltpu.VMEM((seq_a + n_dec, LANES), f32),
                pltpu.VMEM((n_dec + seq_b, LANES), f32),
                pltpu.VMEM((n_dec, d_model // groups), bf),
                pltpu.VMEM((5, nl, n_dec, LANES), bf),
                pltpu.VMEM((ff // LANES, n_dec, LANES), bf),
                pltpu.VMEM((2, n_dec, LANES), f32),
                dma((2 * NSLOT,)), dma((2 * nl,)), dma((nx,)), dma((nx,)), dma((3, n_dev)), dma((stages * n_prompts,)), dma((n_dev,)), dma((n_dev,)), dma((width,)), dma((2,)),
            ],
            compiler_params=pltpu.CompilerParams(collective_id=0, has_side_effects=True, vmem_limit_bytes=67043328),
        )(lengths, cos_t, sin_t, gain_attn, gain_mlp, x_new, x_prompt, st_qkv, st_out, st_gateup, st_down_t)

        picked = res.reshape(width, groups, 4, nx // groups, BLK).transpose(0, 2, 3, 1, 4).reshape(width, 4, d_model)
        last_hidden = jnp.concatenate([picked[:, 0], picked[0::2, 1] + picked[1::2, 1]], axis=0)
        dec_out = jnp.concatenate([picked[:, 2], picked[1::2, 3]], axis=0)

        dec_kv = jnp.concatenate([dec_all[:, :, 0], dec_all[:, 1::2, 1]], axis=1)

        def cache(part):
            own = dec_kv[:, :, part * head_dim:(part + 1) * head_dim]
            return jnp.concatenate([kv_all[:, :, part], own[..., None]], axis=3).transpose(0, 1, 3, 2)[:, :, :, None, :]

        return dec_out, last_hidden, cache(0), cache(1)

    return jax.shard_map(shard_body, mesh=mesh, in_specs=in_specs, out_specs=out_specs, check_vma=False)
```

time: 393 us -> 299 us (0.76)
  Pallas kernels: 367 us -> 289 us
  local copies, waits for them, and re-layouts: 13.6 us -> 5.25 us
  other arithmetic: 9.76 us -> 3.51 us
    pallas_call x1, Pallas kernels: 367 us -> 289 us  [shard_body(): pl.pallas_call(functools.partial(stage_kernel, dims), out_shape=(jax.Shap...]
    slice x6 -> x4, local copies, waits for them, and re-layouts: 6.31 us -> 1.64 us  [shard_body(): dec_kv = jnp.concatenate([dec_all[:, :, 0], dec_all[:, 1::2, 1]], axis=1)]
where the time goes in v2:
time: 299 us
  Pallas kernels  289 us (97%)
  local copies, waits for them, and re-layouts  5.25 us (2%)
  other arithmetic  3.51 us (1%)
    pallas_call x1, Pallas kernels, shard_body(): pl.pallas_call(functools.partial(stage_kernel, dims), out_shape=(jax.Shap...  289 us

profile of v2, /device:TPU:97, one launch (start us, length us, event | category | flops | bytes accessed | tf_op | source)
XLA Modules:
  0.0 298.7 jit_solution(2852780272370389871)
XLA Ops:
  0.6 1.3 copy.40.lens_ref
  2.0 289.2 %shard_map.138 = (bf16[8,6,2,64,128]{4,3,2,1,0:T(8,128)(2,1)}, bf16[8,4,16,128]{3,2,1,0:T(8,128)(2,1)}, bf16[4,16,512]{2,1,0:T(8,128)(2,1)}) custom-call(s32[6,1]{1,0:T(8,128)} %copy.40.lens_ref, f32[136,128]{1,0:T(8,128)} %constant.4.clone.cos_t, f32[136,128]{1,0:T(8,128)} %constant.5.clone.sin_t, f32[8,2048]{1,0:T(8,128)} %ga_ref.1, f32[8,2048]{1,0:T(8,128)} %gm_ref.1, ...), custom_call_target="tpu_custom_call" | custom-call | tf_op jit(solution)/shard_map/pallas_call | solution.py:567
  291.2 0.0 copy-start
  291.2 1.0 reshape.15
  292.4 0.8 slice.40
  293.2 0.9 slice.39
  294.0 0.1 fusion
  294.1 0.7 pad_maximum_fusion
  294.8 0.5 copy.45
  295.3 0.5 copy.44
  295.8 0.0 copy-done
  295.8 0.2 slice_bitcast_fusion
  295.9 2.8 maximum_bitcast_fusion
  (9 shorter events, 0.2 us)
Async XLA Ops:
  291.2 4.6 %copy-start = (bf16[8,6,2,64,128]{4,3,2,1,0:T(8,128)(2,1)S(1)}, bf16[8,6,2,64,128]{4,3,2,1,0:T(8,128)(2,1)}, u32[]{:S(2)}) copy-start(bf16[8,6,2,64,128]{4,3,2,1,0:T(8,128)(2,1)} %get-tuple-element.8) | copy-start | bytes 4718596

commit v3 on v2

v3 whole, which is shorter than its diff:
```python
import functools

import jax
import jax.numpy as jnp
import numpy as np
from jax import lax
from jax.experimental import pallas as pl
from jax.experimental.pallas import tpu as pltpu
from jax.sharding import PartitionSpec as P

EPS = 1e-5
THETA = 10000.0
TP_AXES = ('model', 'model2')
MESH = pl.DeviceIdType.MESH
BLK = 256
LANES = 128
NSLOT = 32
NEG = -1e30
QU = 4
GU = 4


def rope_table(count, head_dim):
    half_dim = head_dim // 2
    inv_freq = np.power(np.float32(THETA), np.arange(half_dim, dtype=np.float32) * np.float32(-2.0 / head_dim))
    angles = (np.arange(count, dtype=np.float32)[:, None] * inv_freq.astype(np.float32)).astype(np.float64)
    cos, sin = np.cos(angles).astype(np.float32), np.sin(angles).astype(np.float32)
    return jnp.asarray(np.tile(cos, (1, 2 * LANES // head_dim))), jnp.asarray(np.tile(np.concatenate([-sin, sin], axis=1), (1, LANES // head_dim)))


def dot_nn(a, b):
    return lax.dot_general(a, b, (((1,), (0,)), ((), ())), preferred_element_type=jnp.float32)


def dot_nt(a, b):
    return lax.dot_general(a, b, (((1,), (1,)), ((), ())), preferred_element_type=jnp.float32)


def cat(ref, first, count):
    return jnp.concatenate([ref[first + t] for t in range(count)], axis=1)


def stage_kernel(dims, lens_ref, cos_t, sin_t, ga_ref, gm_ref, new_ref, x_hbm, w_qkv, w_out, w_gu, w_dt, kv_out, dec_out, res_out,
                 ring, dbuf, xin_a, xin_b, xout_a, xout_b, h_a, h_b, qbuf, x1buf, abuf, kvp_a, kvp_b, kva, kvb, kv_recv, kvt, kvd, tab_a, tab_b, gains, mask_a, mask_b, res_vm, small, asmall, tsmall,
                 ring_sem, d_sem, x0_sem, xs_sem, xr_sem, ks_sem, kr_sem, kd_sem, rs_sem, rr_sem, pair_sem):
    stages, width, kv_heads, head_dim, seq_a, seq_b, n_dec, q_cols, ff, n_prompts = dims
    rows_a, rows_b = seq_a + n_dec, seq_b + n_dec
    d_model = w_out.shape[2]
    nx = d_model // BLK
    nl = d_model // LANES
    nq = q_cols // BLK
    nff = ff // BLK
    n_dev = stages * width
    per_head = stages // kv_heads
    last = stages - 1
    bf, f32 = jnp.bfloat16, jnp.float32
    stage = lax.axis_index('model')
    col = lax.axis_index('model2')
    me = stage * width + col
    half = lax.rem(col, 2)
    shared = width + col // 2
    len_a = lens_ref[col, 0]
    len_b = lens_ref[shared, 0]

    def ring_copy(ref, c, slot, t):
        start = pl.multiple_of(c * BLK + t * LANES, LANES)
        return pltpu.make_async_copy(ref.at[0, :, pl.ds(start, LANES)], ring.at[2 * slot + t], ring_sem.at[2 * slot + t])

    def ring_start(ref, c, slot):
        ring_copy(ref, c, slot, 0).start()
        ring_copy(ref, c, slot, 1).start()

    def wait_slot(slot):
        ring_copy(w_out, 0, slot, 0).wait()
        ring_copy(w_out, 0, slot, 1).wait()

    def weight(slot):
        return cat(ring, 2 * slot, 2)

    order = [(w_qkv, nq), (w_qkv, nq + 1)] + [(w_qkv, c) for c in range(nq)] + [(w_out, c) for c in range(nx)]
    n_attn = len(order)
    for j in range(nff):
        order += [(w_gu, j), (w_gu, nff + j)]
    n_up = len(order)

    def issue(base, i):
        ref, c = order[i % len(order)]
        ring_start(ref, c, (base + i) % NSLOT)

    def x0_copies():
        out = []
        for n in range(nl):
            cs = pl.ds(n * LANES, LANES)
            out.append(pltpu.make_async_copy(x_hbm.at[col, 0, :, cs], xin_a.at[n, pl.ds(0, seq_a), :], x0_sem.at[2 * n]))
            out.append(pltpu.make_async_copy(x_hbm.at[shared, 0, pl.ds(pl.multiple_of(half * seq_b, seq_b), seq_b), cs], xin_b.at[n, pl.ds(0, seq_b), :], x0_sem.at[2 * n + 1]))
        return out

    @pl.when(stage == 0)
    def _():
        for c in x0_copies():
            c.start()

    for i in range(NSLOT):
        issue(0, i)

    def d_copy(k):
        return pltpu.make_async_copy(w_dt.at[0, :, pl.ds(k * LANES, LANES)], dbuf.at[k], d_sem.at[k])

    @pl.when(stage > 0)
    def _():
        for k in range(2 * nff):
            d_copy(k).start()

    barrier = pltpu.get_barrier_semaphore()

    def device(d):
        return {'model': d // width, 'model2': lax.rem(d, width)}

    def greet(i, carry):
        pl.semaphore_signal(barrier, inc=1, device_id=device(lax.rem(me + i, n_dev)), device_id_type=MESH)
        return carry

    lax.fori_loop(1, n_dev, greet, 0)

    for which, ref in ((0, ga_ref), (1, gm_ref)):
        mine = lax.broadcasted_iota(jnp.int32, (ref.shape[0], LANES), 0) == stage
        for n in range(nl):
            gains[which, n, 0:1, :] = jnp.sum(jnp.where(mine, ref[:, n * LANES:(n + 1) * LANES], 0.0), axis=0, keepdims=True)
    row_d = lax.broadcasted_iota(jnp.int32, (n_dec, LANES), 0)
    for k, table in enumerate((cos_t, sin_t)):
        tab_a[k, 0:seq_a, :] = table[0:seq_a, :]
        tab_a[k, seq_a:rows_a, :] = jnp.broadcast_to(table[pl.ds(len_a, 1), :], (n_dec, LANES))
        tab_b[k, 0:seq_b, :] = table[pl.ds(pl.multiple_of(half * seq_b, seq_b), seq_b), :]
        tab_b[k, seq_b:rows_b, :] = jnp.broadcast_to(table[pl.ds(len_b, 1), :], (n_dec, LANES))
    for table, out in ((cos_t, 0), (sin_t, 1)):
        picked = jnp.where(row_d == 0, table[pl.ds(jnp.maximum(len_a - 1, 0), 1), :], table[pl.ds(jnp.maximum(len_b - 1, 0), 1), :])
        picked = jnp.where(row_d == 2, table[pl.ds(len_a, 1), :], picked)
        tsmall[out] = jnp.where(row_d == 3, table[pl.ds(len_b, 1), :], picked)

    def fill_mask(out, rows, offset, length):
        key = lax.broadcasted_iota(jnp.int32, (rows, LANES), 1)
        row = lax.broadcasted_iota(jnp.int32, (rows, LANES), 0) + offset
        out[0:rows, :] = ((key <= row) & (key < length)).astype(f32)
        key = lax.broadcasted_iota(jnp.int32, (n_dec, LANES), 1)
        out[rows:rows + n_dec, :] = (key < length).astype(f32)

    fill_mask(mask_a, seq_a, 0, len_a)
    fill_mask(mask_b, seq_b, half * seq_b, len_b)

    @pl.when(stage == 0)
    def _():
        for n in range(nl):
            for dst, lo, want in ((xin_a, seq_a, col), (xin_b, seq_b, jnp.where(half == 1, shared, -1))):
                acc = jnp.zeros((n_dec, LANES), f32)
                for b in range(n_prompts):
                    acc = acc + jnp.where((row_d == 0) & (want == b), new_ref[b:b + 1, n * LANES:(n + 1) * LANES].astype(f32), 0.0)
                dst[n, lo:lo + n_dec, :] = acc.astype(bf)
        for c in x0_copies():
            c.wait()

    def x_send(k, n):
        two = pl.ds(2 * n, 2)
        src, dst = ((xout_a, xin_a), (xout_b, xin_b))[k]
        return pltpu.make_async_remote_copy(src_ref=src.at[two], dst_ref=dst.at[two], send_sem=xs_sem.at[k, n], recv_sem=xr_sem.at[k, n],
                                            device_id={'model': lax.rem(stage + 1, stages), 'model2': col}, device_id_type=MESH)

    def x_arrive(k):
        @pl.when(stage > 0)
        def _():
            for n in range(nx):
                x_send(k, n).wait_recv()

    def rms_into(src, which, dst):
        ss = jnp.zeros(src.shape[1:], f32)
        for n in range(nl):
            v = src[n].astype(f32)
            ss = ss + v * v
        inv = lax.rsqrt(jnp.sum(ss, axis=-1, keepdims=True) * (1.0 / d_model) + EPS)
        for n in range(nl):
            dst[n] = (src[n].astype(f32) * inv * gains[which, n, 0:1, :]).astype(bf)

    def rope(y, cos, sin):
        lane = lax.broadcasted_iota(jnp.int32, y.shape, 1)
        first_half = lax.rem(lane, head_dim) < head_dim // 2
        swapped = jnp.where(first_half, pltpu.roll(y, LANES - head_dim // 2, 1), pltpu.roll(y, head_dim // 2, 1))
        return y * cos + swapped * sin

    def keys_values(src, tab, dst, slot):
        h = cat(src, 0, nl)
        k_all = dot_nn(h, weight(slot))
        v_all = dot_nn(h, weight(lax.rem(slot + 1, NSLOT)))
        low = lax.broadcasted_iota(jnp.int32, (src.shape[1], LANES), 1) < head_dim
        for c in range(kv_heads):
            p = c // 2
            kk = rope(k_all[:, p * LANES:(p + 1) * LANES], tab[0], tab[1])
            vv = v_all[:, p * LANES:(p + 1) * LANES]
            if c % 2 == 0:
                packed = jnp.where(low, kk, pltpu.roll(vv, head_dim, 1))
            else:
                packed = jnp.where(low, pltpu.roll(kk, head_dim, 1), vv)
            dst[c] = packed.astype(bf)

    def pair_copy():
        return pltpu.make_async_remote_copy(src_ref=kvp_b.at[:, pl.ds(0, seq_b), :], dst_ref=kv_recv, send_sem=pair_sem.at[0], recv_sem=pair_sem.at[1],
                                            device_id={'model': stage, 'model2': col + 1 - 2 * half}, device_id_type=MESH)

    def queries(base, src, dst, cos, sin):
        def q_step(it, carry):
            sl = [lax.rem(base + 2 + QU * it + r, NSLOT) for r in range(QU)]
            for t in sl:
                wait_slot(t)
            h = cat(src, 0, nl)
            qs = [dot_nn(h, weight(t)) for t in sl]
            for r in range(QU):
                for p in range(2):
                    dst[2 * (QU * it + r) + p] = rope(qs[r][:, p * LANES:(p + 1) * LANES], cos[...], sin[...]).astype(bf)
            return carry

        lax.fori_loop(0, nq // QU, q_step, 0)
        for i in range(NSLOT, NSLOT + nq + 2):
            issue(base, i)

    low_s = lax.broadcasted_iota(jnp.int32, (seq_a, LANES), 1) < head_dim

    def widen(src, dst, c):
        f = src.astype(f32)
        r = pltpu.roll(f, head_dim, 1)
        dst[c, 0, 0:seq_a, :] = jnp.where(low_s, f, 0.0).astype(bf)
        dst[c, 0, seq_a:2 * seq_a, :] = jnp.where(low_s, 0.0, r).astype(bf)
        dst[c, 1, 0:seq_a, :] = jnp.where(low_s, r, 0.0).astype(bf)
        dst[c, 1, seq_a:2 * seq_a, :] = jnp.where(low_s, 0.0, f).astype(bf)

    def widen_b():
        for c in range(kv_heads):
            own_b = kvp_b[c, 0:seq_b, :]

            @pl.when(half == 0)
            def _():
                kvb[c, 2, 0:seq_b, :] = own_b

            @pl.when(half == 1)
            def _():
                kvb[c, 2, 0:seq_b, :] = kv_recv[c]

            kvb[c, 2, seq_b:2 * seq_b, :] = own_b
            widen(kvb[c, 2, 0:seq_a, :], kvb, c)

    def kv_copy(d, which, src_stage, prompt):
        return pltpu.make_async_remote_copy(src_ref=kvt.at[d // (per_head * width), which], dst_ref=kv_out.at[src_stage, prompt], send_sem=ks_sem.at[which, d],
                                            recv_sem=kr_sem.at[src_stage * n_prompts + prompt], device_id=device(d), device_id_type=MESH)

    def kv_local(which, prompt):
        return pltpu.make_async_copy(kvt.at[stage // per_head, which], kv_out.at[stage, prompt], ks_sem.at[which, me])

    def dec_copy(d, src_stage, src_col):
        return pltpu.make_async_remote_copy(src_ref=kvd.at[d // (per_head * width)], dst_ref=dec_out.at[src_stage, src_col], send_sem=ks_sem.at[2, d],
                                            recv_sem=kd_sem.at[src_stage * width + src_col], device_id=device(d), device_id_type=MESH)

    def dec_local():
        return pltpu.make_async_copy(kvd.at[stage // per_head], dec_out.at[stage, col], ks_sem.at[2, me])

    def kv_fill(which, src):
        for c in range(kv_heads):
            t = src(c).astype(f32).T
            for part in range(2):
                kvt[c, which, part] = t[part * head_dim:(part + 1) * head_dim].astype(bf)

    def others(step):
        def body(i, carry):
            step(lax.rem(me + i, n_dev))
            return carry

        lax.fori_loop(1, n_dev, body, 0)

    def emit_a():
        kv_fill(0, lambda c: kvp_a[c, 0:seq_a, :])
        others(lambda d: kv_copy(d, 0, stage, col).start())
        kv_local(0, col).start()

    def emit_b():
        for c in range(kv_heads):
            other = pltpu.roll(kvp_b[c, seq_b:rows_b, :].astype(f32), 1, 0)
            kvd[c] = jnp.where(row_d == 0, kvp_a[c, seq_a:rows_a, :].astype(f32), other).astype(bf)
        others(lambda d: dec_copy(d, stage, col).start())
        dec_local().start()

        @pl.when(half == 1)
        def _():
            kv_fill(1, lambda c: kvb[c, 2, 0:seq_a, :])
            others(lambda d: kv_copy(d, 1, stage, shared).start())
            kv_local(1, shared).start()

    scale = head_dim ** -0.5
    low_d = lax.broadcasted_iota(jnp.int32, (n_dec, LANES), 1) < head_dim

    def soft(s, mask):
        s = jnp.where(mask > 0, s * scale, NEG)
        m = jnp.max(s, axis=-1, keepdims=True)
        e = jnp.exp(s - m)
        return (e * (1.0 / jnp.sum(e, axis=-1, keepdims=True))).astype(bf)

    def soft_self(s, mask, s_self):
        s = jnp.where(mask > 0, s * scale, NEG)
        m = jnp.maximum(jnp.max(s, axis=-1, keepdims=True), s_self)
        e = jnp.exp(s - m)
        e_self = jnp.exp(s_self - m)
        inv = 1.0 / (jnp.sum(e, axis=-1, keepdims=True) + e_self)
        return (e * inv).astype(bf), (e_self * inv).astype(bf).astype(f32)

    pairs_per_kv = q_cols // (kv_heads * LANES)

    def attend(kvp, kv, mask, n_main, dst):
        n_all = n_main + n_dec

        def kv_head(c, carry):
            kv_d = kvp[c, n_main:n_all, :].astype(f32)
            kv_r = pltpu.roll(kv_d, head_dim, 1)
            k_self = jnp.where(low_d, kv_d, kv_r)
            v_self = jnp.where(low_d, kv_r, kv_d)
            for t in range(pairs_per_kv):
                hp = c * pairs_per_kv + t
                prod = qbuf[hp, n_main:n_all, :].astype(f32) * k_self
                self_e = jnp.sum(jnp.where(low_d, prod, 0.0), axis=-1, keepdims=True) * scale
                self_o = jnp.sum(jnp.where(low_d, 0.0, prod), axis=-1, keepdims=True) * scale
                sc = dot_nt(qbuf[hp, 0:n_all, :], kv[c, 0])
                mm, md = mask[0:n_main, :], mask[n_main:n_all, :]
                pm = jnp.concatenate([soft(sc[:n_main, :seq_a], mm), soft(sc[:n_main, seq_a:], mm)], axis=1)
                de, de_s = soft_self(sc[n_main:, :seq_a], md, self_e)
                do, do_s = soft_self(sc[n_main:, seq_a:], md, self_o)
                o = dot_nn(jnp.concatenate([pm, jnp.concatenate([de, do], axis=1)], axis=0), kv[c, 1])
                dst[hp, 0:n_main, :] = o[:n_main].astype(bf)
                dst[hp, n_main:n_all, :] = (o[n_main:] + jnp.where(low_d, de_s, do_s) * v_self).astype(bf)
            return carry

        lax.fori_loop(0, kv_heads, kv_head, 0)

    def project(base, src, res, dst):
        def out_step(it, carry):
            sl = [lax.rem(base + nq + 2 + QU * it + r, NSLOT) for r in range(QU)]
            for t in sl:
                wait_slot(t)
            o = cat(src, 0, nl)
            ys = [dot_nn(o, weight(t)) for t in sl]
            for r in range(QU):
                for p in range(2):
                    n = 2 * (QU * it + r) + p
                    dst[n] = (res[n].astype(f32) + ys[r][:, p * LANES:(p + 1) * LANES]).astype(bf)
            return carry

        lax.fori_loop(0, nx // QU, out_step, 0)
        for i in range(NSLOT + nq + 2, NSLOT + n_attn):
            issue(base, i)

    n_loop = nff // GU * GU

    def gate_up(base, src, dst, again):
        def some(pairs):
            for j, sg in pairs:
                wait_slot(sg)
                wait_slot(lax.rem(sg + 1, NSLOT))
            h = cat(src, 0, nl)
            for j, sg in pairs:
                g = dot_nn(h, weight(sg))
                u = dot_nn(h, weight(lax.rem(sg + 1, NSLOT)))
                a = (g * (1.0 / (1.0 + jnp.exp(-g))) * u).astype(bf)
                dst[2 * j] = a[:, :LANES]
                dst[2 * j + 1] = a[:, LANES:]

        def gu_step(it, carry):
            some([(GU * it + r, lax.rem(base + n_attn + 2 * (GU * it + r), NSLOT)) for r in range(GU)])

            for k in range(n_loop // GU):
                todo = [i for i in range(NSLOT + n_attn + 2 * GU * k, NSLOT + n_attn + 2 * GU * (k + 1)) if again or i < len(order)]
                if todo:
                    @pl.when(it == k)
                    def _(todo=todo):
                        for i in todo:
                            issue(base, i)
            return carry

        lax.fori_loop(0, n_loop // GU, gu_step, 0)
        for lo in range(n_loop, nff, GU):
            some([(j, jnp.int32((base + n_attn + 2 * j) % NSLOT)) for j in range(lo, min(lo + GU, nff))])
        if again:
            for i in range(NSLOT + n_attn + 2 * n_loop, NSLOT + n_up):
                issue(base, i)

    def down(src, res, dst, k_send, flipped):
        def down_step(n, carry):
            ys = []
            for t in range(2):
                lo = pl.multiple_of((2 * n + t) * BLK, BLK)
                acc = None
                for k in range(nff):
                    if flipped:
                        r0, r1 = pl.ds(lo, LANES), pl.ds(pl.multiple_of(lo + LANES, LANES), LANES)
                        w = jnp.concatenate([jnp.concatenate([dbuf[2 * k + i, r0, :], dbuf[2 * k + i, r1, :]], axis=1) for i in range(2)], axis=0)
                        y = dot_nn(cat(src, 2 * k, 2), w)
                    else:
                        rows = pl.ds(lo, BLK)
                        y = dot_nt(cat(src, 2 * k, 2), jnp.concatenate([dbuf[2 * k, rows, :], dbuf[2 * k + 1, rows, :]], axis=1))
                    acc = y if acc is None else acc + y
                ys.append(acc)
            for t in range(2):
                for p in range(2):
                    i = 2 * (2 * n + t) + p
                    dst[i] = (res[i].astype(f32) + ys[t][:, p * LANES:(p + 1) * LANES]).astype(bf)
            if k_send is not None:
                x_send(k_send, 2 * n).start()
                x_send(k_send, 2 * n + 1).start()
            return carry

        lax.fori_loop(0, nx // 2, down_step, 0)

    @pl.when(stage > 0)
    def _():
        for k in range(2 * nff):
            d_copy(k).wait()

        def flip(k, carry):
            for i in range(nl):
                tile = slice(i * LANES, (i + 1) * LANES)
                dbuf[k, tile, :] = dbuf[k, tile, :].astype(f32).T.astype(bf)
            return carry

        lax.fori_loop(0, 2 * nff, flip, 0)

    wait_slot(0)
    wait_slot(1)
    x_arrive(0)
    rms_into(xin_a, 0, h_a)
    keys_values(h_a, tab_a, kvp_a, 0)
    for c in range(kv_heads):
        widen(kvp_a[c, 0:seq_a, :], kva, c)
    part_a, part_b = pl.ds(0, rows_a), pl.ds(0, rows_b)

    @pl.when(stage < last)
    def _():
        q_a = qbuf.at[:, part_a, :]
        queries(0, h_a, q_a, tab_a.at[0], tab_a.at[1])
        attend(kvp_a, kva, mask_a, seq_a, h_a)
        project(0, h_a, xin_a, x1buf.at[:, part_a, :])

        @pl.when(stage == 0)
        def _():
            for k in range(2 * nff):
                d_copy(k).start()

    pl.semaphore_wait(barrier, n_dev - 1)

    @pl.when(stage < last)
    def _():
        rms_into(x1buf.at[:, part_a, :], 1, h_a)
        gate_up(0, h_a, abuf.at[:, part_a, :], True)
        @pl.when(stage == 0)
        def _():
            for k in range(2 * nff):
                d_copy(k).wait()
            down(abuf.at[:, part_a, :], x1buf.at[:, part_a, :], xout_a, 0, False)

        @pl.when(stage > 0)
        def _():
            down(abuf.at[:, part_a, :], x1buf.at[:, part_a, :], xout_a, 0, True)

    second = len(order)
    kv_slot = jnp.where(stage < last, second % NSLOT, 0)

    @pl.when(stage < last)
    def _():
        wait_slot(second % NSLOT)
        wait_slot((second + 1) % NSLOT)

    x_arrive(1)
    rms_into(xin_b, 0, h_b)
    keys_values(h_b, tab_b, kvp_b, kv_slot)

    @pl.when(half == 0)
    def _():
        pair_copy().start()

    @pl.when(stage < last)
    def _():
        queries(second, h_b, qbuf.at[:, part_b, :], tab_b.at[0], tab_b.at[1])

    @pl.when(stage == last)
    def _():
        emit_a()

    @pl.when(half == 1)
    def _():
        pair_copy().wait_recv()

    widen_b()

    @pl.when(stage < last)
    def _():
        attend(kvp_b, kvb, mask_b, seq_b, h_b)
        project(second, h_b, xin_b, x1buf.at[:, part_b, :])
        rms_into(x1buf.at[:, part_b, :], 1, h_b)
        gate_up(second, h_b, abuf.at[:, part_b, :], False)
        @pl.when(stage == 0)
        def _():
            down(abuf.at[:, part_b, :], x1buf.at[:, part_b, :], xout_b, 1, False)

        @pl.when(stage > 0)
        def _():
            down(abuf.at[:, part_b, :], x1buf.at[:, part_b, :], xout_b, 1, True)

        emit_a()
        emit_b()

    def res_copy(d, src_col):
        return pltpu.make_async_remote_copy(src_ref=res_vm, dst_ref=res_out.at[src_col], send_sem=rs_sem.at[d], recv_sem=rr_sem.at[src_col],
                                            device_id=device(d), device_id_type=MESH)

    def res_local():
        return pltpu.make_async_copy(res_vm, res_out.at[col], rs_sem.at[me])

    groups = n_dec // 4

    @pl.when(stage == last)
    def _():
        xs, hs, qs, x1s, ys = (small.at[i] for i in range(5))
        off_b = len_b - 1 - half * seq_b

        def one_hot(rows, first, last_row, dec_row, dec_on):
            who = lax.broadcasted_iota(jnp.int32, (n_dec, rows), 0)
            at = lax.broadcasted_iota(jnp.int32, (n_dec, rows), 1)
            hit = ((who == first) & (at < dec_row) & (at == last_row)) | ((who == first + 2) & dec_on & (at == dec_row))
            return jnp.where(hit, 1.0, 0.0).astype(bf)

        sel_a = one_hot(rows_a, 0, len_a - 1, seq_a, stage == last)
        sel_b = one_hot(rows_b, 1, off_b, seq_b, half == 1)
        for n in range(nl // 2):
            for src_a, src_b, dst in ((xin_a, xin_b, xs), (h_a, h_b, hs)):
                y = (dot_nn(sel_a, cat(src_a, 2 * n, 2)) + dot_nn(sel_b, cat(src_b, 2 * n, 2))).astype(bf)
                dst[2 * n] = y[:, :LANES]
                dst[2 * n + 1] = y[:, LANES:]
        queries(0, hs, qs, tsmall.at[0], tsmall.at[1])
        emit_b()

        stack = pairs_per_kv * n_dec
        key = lax.broadcasted_iota(jnp.int32, (stack, LANES), 1)
        row = lax.rem(lax.broadcasted_iota(jnp.int32, (stack, LANES), 0), n_dec)
        low_k = key < head_dim
        mk_a, mk_b = (key < len_a).astype(f32), (key < len_b).astype(f32)
        decode = (row[:, 0:1] == 2) | (row[:, 0:1] == 3)
        from_a = lax.rem(row, 2) == 0
        for c in range(kv_heads):
            kd = kvd[c].astype(f32)
            kr = pltpu.roll(kd, head_dim, 1)
            k_two, v_two = jnp.where(low_d, kd, kr), jnp.where(low_d, kr, kd)
            k_self = jnp.where(from_a, k_two[0:1], k_two[1:2])
            v_self = jnp.where(from_a, v_two[0:1], v_two[1:2])
            q4 = jnp.concatenate([qs[c * pairs_per_kv + t] for t in range(pairs_per_kv)], axis=0)
            prod = q4.astype(f32) * k_self
            self_e = jnp.where(decode, jnp.sum(jnp.where(low_k, prod, 0.0), axis=-1, keepdims=True) * scale, NEG)
            self_o = jnp.where(decode, jnp.sum(jnp.where(low_k, 0.0, prod), axis=-1, keepdims=True) * scale, NEG)
            outs = []
            for kv, mk in ((kva, mk_a), (kvb, mk_b)):
                sc = dot_nt(q4, kv[c, 0])
                pe, pe_s = soft_self(sc[:, :seq_a], mk, self_e)
                po, po_s = soft_self(sc[:, seq_a:], mk, self_o)
                outs.append(dot_nn(jnp.concatenate([pe, po], axis=1), kv[c, 1]) + jnp.where(low_k, pe_s, po_s) * v_self)
            o = jnp.where(from_a, outs[0], outs[1]).astype(bf)
            for t in range(pairs_per_kv):
                hs[c * pairs_per_kv + t] = o[t * n_dec:(t + 1) * n_dec]

        project(0, hs, xs, x1s)
        rms_into(x1s, 1, hs)
        gate_up(0, hs, asmall, False)
        down(asmall, x1s, ys, None, True)
        keep = (row_d == 0) | (row_d == 2) | ((row_d == 1) & (off_b >= 0) & (off_b < seq_b)) | ((row_d == 3) & (half == 1))
        for n in range(2 * nx // groups):
            j, p = n // 2, n % 2
            acc = jnp.zeros((n_dec, LANES), f32)
            for i in range(groups):
                y = jnp.where(keep, ys[2 * (groups * j + i) + p].astype(f32), 0.0)
                y = pltpu.roll(y, 4 * i, 0) if i else y
                acc = jnp.where(row_d // 4 == i, y, acc)
            res_vm[:, n * LANES:(n + 1) * LANES] = acc.astype(bf)
        others(lambda d: res_copy(d, col).start())
        res_local().start()
        others(lambda d: res_copy(d, col).wait_send())
        res_local().wait()

    @pl.when(stage < last)
    def _():
        for k in range(2):
            for n in range(nx):
                x_send(k, n).wait_send()

    @pl.when(half == 0)
    def _():
        pair_copy().wait_send()

    others(lambda d: dec_copy(d, stage, col).wait_send())
    dec_local().wait()
    others(lambda d: kv_copy(d, 0, stage, col).wait_send())
    kv_local(0, col).wait()

    @pl.when(half == 1)
    def _():
        others(lambda d: kv_copy(d, 1, stage, shared).wait_send())
        kv_local(1, shared).wait()

    others(lambda d: dec_copy(0, d // width, lax.rem(d, width)).wait_recv())
    for b in range(n_prompts):
        owner = b if b < width else 2 * (b - width) + 1

        def kv_in(s, carry, b=b, owner=owner):
            @pl.when((s != stage) | (col != owner))
            def _():
                kv_copy(0, 0, s, b).wait_recv()
            return carry

        lax.fori_loop(0, stages, kv_in, 0)

    def res_in(y, carry):
        @pl.when((stage != last) | (y != col))
        def _():
            res_copy(0, y).wait_recv()
        return carry

    lax.fori_loop(0, width, res_in, 0)


def solution(mesh):
    stages = mesh.shape['model']
    width = mesh.shape['model2']
    stage_spec = P('model', None, None)
    in_specs = (P('replica', None, None, None), P('replica', None), P('replica', None),
                stage_spec, stage_spec, stage_spec, stage_spec, P(None, None), P(None, None),
                P(None, None, TP_AXES, None), P(None, None, TP_AXES, None), P(None, None, TP_AXES, None),
                P(None, TP_AXES, None, None), P(None, None, TP_AXES), P(None, None, TP_AXES), P(None, TP_AXES, None))
    cache_spec = P(None, 'replica', None, TP_AXES, None)
    out_specs = (P('replica', None), P('replica', None), cache_spec, cache_spec)

    def shard_body(x_prompt, lengths, x_new, st_qkv, st_out, st_gateup, st_down_t, gain_attn, gain_mlp, tp_query, tp_key, tp_value, tp_out, tp_gate, tp_up, tp_down):
        n_prompts, _, seq_len, d_model = x_prompt.shape
        head_dim = tp_query.shape[-1]
        q_cols = st_out.shape[1]
        kv_heads = (st_qkv.shape[2] - q_cols) // (2 * head_dim)
        ff = st_down_t.shape[2]
        n_dec = 16
        seq_a, seq_b = seq_len, seq_len // 2
        assert n_prompts == width + width // 2 and st_qkv.shape[0] == 1 and tp_key.shape[2] == 1
        rows_a, rows_b = seq_a + n_dec, seq_b + n_dec
        groups = n_dec // 4
        bf, f32 = jnp.bfloat16, jnp.float32
        cos_t, sin_t = rope_table(seq_len + 8, head_dim)
        dims = (stages, width, kv_heads, head_dim, seq_a, seq_b, n_dec, q_cols, ff, n_prompts)
        nx, nl = d_model // BLK, d_model // LANES
        n_dev = stages * width
        vmem, hbm = pl.BlockSpec(memory_space=pltpu.VMEM), pl.BlockSpec(memory_space=pl.ANY)
        smem = pl.BlockSpec(memory_space=pltpu.SMEM)
        dma = pltpu.SemaphoreType.DMA
        kv_all, dec_all, res = pl.pallas_call(
            functools.partial(stage_kernel, dims),
            out_shape=(jax.ShapeDtypeStruct((stages, n_prompts, 2, head_dim, seq_len), bf), jax.ShapeDtypeStruct((stages, width, n_dec, LANES), bf), jax.ShapeDtypeStruct((width, n_dec, d_model // groups), bf)),
            in_specs=[smem] + [vmem] * 5 + [hbm] * 5,
            out_specs=(hbm, hbm, hbm),
            scratch_shapes=[
                pltpu.VMEM((2 * NSLOT, d_model, LANES), bf),
                pltpu.VMEM((ff // LANES, d_model, LANES), bf),
                pltpu.VMEM((nl, rows_a, LANES), bf),
                pltpu.VMEM((nl, rows_b, LANES), bf),
                pltpu.VMEM((nl, rows_a, LANES), bf),
                pltpu.VMEM((nl, rows_b, LANES), bf),
                pltpu.VMEM((nl, rows_a, LANES), bf),
                pltpu.VMEM((nl, rows_b, LANES), bf),
                pltpu.VMEM((q_cols // LANES, rows_a, LANES), bf),
                pltpu.VMEM((nl, rows_a, LANES), bf),
                pltpu.VMEM((ff // LANES, rows_a, LANES), bf),
                pltpu.VMEM((kv_heads, rows_a, LANES), bf),
                pltpu.VMEM((kv_heads, rows_b, LANES), bf),
                pltpu.VMEM((kv_heads, 2, 2 * seq_a, LANES), bf),
                pltpu.VMEM((kv_heads, 3, 2 * seq_a, LANES), bf),
                pltpu.VMEM((kv_heads, seq_b, LANES), bf),
                pltpu.VMEM((kv_heads, 2, 2, head_dim, seq_len), bf),
                pltpu.VMEM((kv_heads, n_dec, LANES), bf),
                pltpu.VMEM((2, rows_a, LANES), f32),
                pltpu.VMEM((2, rows_b, LANES), f32),
                pltpu.VMEM((2, nl, 8, LANES), f32),
                pltpu.VMEM((rows_a, LANES), f32),
                pltpu.VMEM((rows_b, LANES), f32),
                pltpu.VMEM((n_dec, d_model // groups), bf),
                pltpu.VMEM((5, nl, n_dec, LANES), bf),
                pltpu.VMEM((ff // LANES, n_dec, LANES), bf),
                pltpu.VMEM((2, n_dec, LANES), f32),
                dma((2 * NSLOT,)), dma((ff // LANES,)), dma((2 * nl,)), dma((2, nx)), dma((2, nx)), dma((3, n_dev)), dma((stages * n_prompts,)), dma((n_dev,)), dma((n_dev,)), dma((width,)), dma((2,)),
            ],
            compiler_params=pltpu.CompilerParams(collective_id=0, has_side_effects=True, vmem_limit_bytes=67043328),
        )(lengths, cos_t, sin_t, gain_attn, gain_mlp, x_new, x_prompt, st_qkv, st_out, st_gateup, st_down_t)

        picked = res.reshape(width, groups, 4, nx // groups, BLK).transpose(0, 2, 3, 1, 4).reshape(width, 4, d_model)
        last_hidden = jnp.concatenate([picked[:, 0], picked[0::2, 1] + picked[1::2, 1]], axis=0)
        dec_out = jnp.concatenate([picked[:, 2], picked[1::2, 3]], axis=0)

        dec_kv = jnp.concatenate([dec_all[:, :, 0], dec_all[:, 1::2, 1]], axis=1)

        def cache(part):
            own = dec_kv[:, :, part * head_dim:(part + 1) * head_dim]
            return jnp.concatenate([kv_all[:, :, part], own[..., None]], axis=3).transpose(0, 1, 3, 2)[:, :, :, None, :]

        return dec_out, last_hidden, cache(0), cache(1)

    return jax.shard_map(shard_body, mesh=mesh, in_specs=in_specs, out_specs=out_specs, check_vma=False)
```

time: 299 us -> 264 us (0.88)
  Pallas kernels: 289 us -> 255 us
    pallas_call x1, Pallas kernels: 289 us -> 255 us  [shard_body(): pl.pallas_call(functools.partial(stage_kernel, dims), out_shape=(jax.Shap...]
where the time goes in v3:
time: 264 us
  Pallas kernels  255 us (97%)
  local copies, waits for them, and re-layouts  5.25 us (2%)
  other arithmetic  3.51 us (1%)
    pallas_call x1, Pallas kernels, shard_body(): pl.pallas_call(functools.partial(stage_kernel, dims), out_shape=(jax.Shap...  255 us

profile of v3, /device:TPU:97, one launch (start us, length us, event | category | flops | bytes accessed | tf_op | source)
XLA Modules:
  0.0 264.2 jit_solution(11116594956190711452)
XLA Ops:
  0.6 1.3 copy.40.lens_ref
  2.0 254.7 %shard_map.138 = (bf16[8,6,2,64,128]{4,3,2,1,0:T(8,128)(2,1)}, bf16[8,4,16,128]{3,2,1,0:T(8,128)(2,1)}, bf16[4,16,512]{2,1,0:T(8,128)(2,1)}) custom-call(s32[6,1]{1,0:T(8,128)} %copy.40.lens_ref, f32[136,128]{1,0:T(8,128)} %constant.4.clone.cos_t, f32[136,128]{1,0:T(8,128)} %constant.5.clone.sin_t, f32[8,2048]{1,0:T(8,128)} %ga_ref.1, f32[8,2048]{1,0:T(8,128)} %gm_ref.1, ...), custom_call_target="tpu_custom_call" | custom-call | tf_op jit(solution)/shard_map/pallas_call | solution.py:658
  256.7 0.0 copy-start
  256.7 1.0 reshape.15
  257.9 0.8 slice.40
  258.6 0.9 slice.39
  259.5 0.1 fusion
  259.6 0.7 pad_maximum_fusion
  260.3 0.5 copy.45
  260.8 0.5 copy.44
  261.3 0.0 copy-done
  261.3 0.2 slice_bitcast_fusion
  261.4 2.8 %maximum_bitcast_fusion = (bf16[8,6,129,1,64]{2,4,3,1,0:T(8,128)(2,1)}, bf16[8,6,129,1,64]{2,4,3,1,0:T(8,128)(2,1)}) fusion(bf16[8,6,64,1]{3,2,1,0:T(8,128)(2,1)S(1)} %copy.44, bf16[8,6,64,128]{3,2,1,0:T(8,128)(2,1)S(1)} %get-tuple-element.27, bf16[8,6,64,1]{3,2,1,0:T(8,128)(2,1)S(1)} %copy.45, bf16[8,6,64,128]{3,2,1,0:T(8,128)(2,1)S(1)} %get-tuple-element.26), kind=kLoop, calls=%fused_computation | loop fusion | flops 3170304 | bytes 3170304
  (9 shorter events, 0.2 us)
Async XLA Ops:
  256.7 4.6 %copy-start = (bf16[8,6,2,64,128]{4,3,2,1,0:T(8,128)(2,1)S(1)}, bf16[8,6,2,64,128]{4,3,2,1,0:T(8,128)(2,1)}, u32[]{:S(2)}) copy-start(bf16[8,6,2,64,128]{4,3,2,1,0:T(8,128)(2,1)} %get-tuple-element.8) | copy-start | bytes 4718596
